TPU v7x, 32 devices: a whole 2x2x4 slice. The times are simulated.
32 devices in a mesh: chan: 4 (over x, core), slab: 8 (over z, y).
Axes of the slice: x: 2, y: 2, z: 4, core: 2. Of those that a mesh axis runs over, the one named last changes fastest.
Arguments:
- beam_images: float32 [64, 512, 4096], P('chan', 'slab'), may hold values from -24 to 24
- chan_weights: int32 [64], P('chan'), may hold values from 1 to 8
- freq_offsets: float32 [64], P('chan'), may hold values from -1 to 1
- half_widths: int32 [5], replicated, may hold values from 16 to 32, as said below
Outputs:
- smoothed: float32 [5, 512, 4096], P(None, 'slab', 'chan')
Inputs may be any that keep to these rules, and one draw needn't show every extreme that they name: `half_widths`: each half-width is at least 16 and at most 32; at least one equals 32.
All inputs are finite; a program needn't handle non-finite values.
Results may differ from a plain program's by a relative error of at most 0.00008.
Values sent between devices are 32-bit elements; how exact they have to be, the bound alone decides.
No kernel may reach another device: no remote copies, remote signals or barrier semaphores. Data moves between devices by JAX's collectives and lax.ppermute only.
A program may use at most 128 MiB of HBM per device.

v0:
```python
import jax
import jax.numpy as jnp
from jax import lax
from jax.sharding import PartitionSpec as P

MOMENTS = 5
HW_MAX = 32


def padded(cells, sides, width):
    for axis, dim in sides:
        count = lax.axis_size(axis)
        ends = count - 1
        head = lax.slice_in_dim(cells, 0, width, axis=dim)
        tail = lax.slice_in_dim(cells, cells.shape[dim] - width, cells.shape[dim], axis=dim)
        cells = jnp.concatenate(
            [
                lax.ppermute(tail, axis, [(i, (i + 1) % count) for i in range(ends)]),
                cells,
                lax.ppermute(head, axis, [((i + 1) % count, i) for i in range(ends)]),
            ],
            axis=dim,
        )
    return cells


def row_pass(extended, half_widths):
    total_rows = extended.shape[1]
    out_rows = total_rows - 2 * HW_MAX
    out_index = lax.broadcasted_iota(jnp.int32, (out_rows, total_rows), 0)
    in_index = lax.broadcasted_iota(jnp.int32, (out_rows, total_rows), 1)
    distance = jnp.abs(in_index - HW_MAX - out_index)
    row_band = (distance[None] <= half_widths[:, None, None]).astype(jnp.float32)
    return jnp.einsum(
        "kim,kmj->kij",
        row_band,
        extended,
        precision=lax.Precision.HIGHEST,
        preferred_element_type=jnp.float32,
    )


def column_pass(extended, half_widths):
    total_cols = extended.shape[2]
    out_cols = total_cols - 2 * HW_MAX
    in_index = lax.broadcasted_iota(jnp.int32, (total_cols, out_cols), 0)
    out_index = lax.broadcasted_iota(jnp.int32, (total_cols, out_cols), 1)
    distance = jnp.abs(in_index - HW_MAX - out_index)
    col_band = (distance[None] <= half_widths[:, None, None]).astype(jnp.float32)
    return jnp.einsum(
        "kim,kmj->kij",
        extended,
        col_band,
        precision=lax.Precision.HIGHEST,
        preferred_element_type=jnp.float32,
    )


def body(beam_images, chan_weights, freq_offsets, half_widths):
    local_chans = beam_images.shape[0]
    slab_rows = beam_images.shape[1]
    all_cols = beam_images.shape[2]
    weight_floats = chan_weights.astype(jnp.float32)
    weight_total = lax.psum(jnp.sum(weight_floats), "chan")
    powers = jnp.stack([freq_offsets**power for power in range(MOMENTS)])
    coefficients = powers * weight_floats[None, :] / weight_total
    flat = beam_images.reshape(local_chans, slab_rows * all_cols)
    partials = jnp.dot(
        coefficients, flat, precision=lax.Precision.HIGHEST, preferred_element_type=jnp.float32
    )
    partials = partials.reshape(MOMENTS, slab_rows, all_cols)
    shares = lax.psum_scatter(partials, "chan", scatter_dimension=2, tiled=True)
    extended = padded(shares, (("chan", 2), ("slab", 1)), HW_MAX)
    summed = column_pass(row_pass(extended, half_widths), half_widths)
    divisor = (2 * half_widths + 1).astype(jnp.float32)
    return summed / divisor[:, None, None]


def solution(mesh):
    placed = (P("chan", "slab", None), P("chan"), P("chan"), P())
    return jax.shard_map(
        body, mesh=mesh, in_specs=placed, out_specs=P(None, "slab", "chan"), check_vma=False
    )
```

profile of v0, /device:TPU:12, one launch (start us, length us, event | category | flops | bytes accessed | tf_op | source)
XLA Modules:
  0.0 181.0 jit_solution(14142702040330019282)
XLA Ops:
  6.5 0.0 reduce-scatter.2.cloned.1.call-start
  6.5 0.7 multiply_bitcast_fusion
  7.2 1.3 convert_reduce_fusion
  8.5 0.7 convert_element_type.8
  9.1 7.5 %psum.7 = f32[]{:T(128)} all-reduce(f32[]{:T(128)} %convert_reduce_fusion), channel_id=1, replica_groups=mesh['chan'=4,'slab'=8] {'chan'}, use_global_device_ids=true, to_apply=%region_1.0 | all-reduce | flops 1 | bytes 8 | tf_op jit(solution)/shard_map/psum | solution.py:64
  16.6 0.7 stack.19
  17.3 25.8 %fusion.2 = f32[5,64,4096]{2,0,1:T(8,128)} fusion(f32[5,16]{1,0:T(8,128)S(1)} %stack.19, f32[]{:T(128)} %psum.7, f32[16]{0:T(128)S(1)} %convert_element_type.8, f32[2,8,64,4096]{3,2,1,0:T(8,128)} %bitcast.22), kind=kOutput, calls=%fused_computation.2 | convolution fusion | flops 251658400 | bytes 22020484 | tf_op jit(solution)/shard_map/dot_general | solution.py:68
  43.1 0.0 copy-start
  43.1 0.0 reduce-scatter.2.cloned.1.call-update
  43.2 71.6 %reduce-scatter.2.cloned.1.call-done = f32[5,64,1024]{2,0,1:T(8,128)} async-done(((f32[5,64,4096]{2,0,1:T(8,128)}), f32[5,64,1024]{2,0,1:T(8,128)}) %reduce-scatter.2.cloned.1.call-update) | async-done | bytes 1310736 | tf_op jit(solution)/shard_map/reduce_scatter | solution.py:72
  114.7 1.2 fusion.21
  115.9 1.6 collective-permute-start
  117.5 1.3 collective-permute-start.1
  118.8 0.0 copy-done
  118.8 0.0 collective-permute-done
  118.8 2.6 %collective-permute-done.1 = f32[5,64,32]{2,0,1:T(8,128)S(1)} collective-permute-done((f32[5,64,32]{2,0,1:T(8,128)S(1)}, f32[5,64,32]{2,0,1:T(8,128)S(1)}, u32[]{:S(2)}, u32[]{:S(2)}) %collective-permute-start.1) | collective-permute-done | bytes 40992 | tf_op jit(solution)/shard_map/ppermute | solution.py:20
  121.4 3.1 %concatenate.6 = f32[5,64,1088]{2,0,1:T(8,128)S(1)} concatenate(f32[5,64,32]{2,0,1:T(8,128)S(1)} %collective-permute-done, f32[5,64,1024]{2,0,1:T(8,128)} %reduce-scatter.2.cloned.1.call-done, f32[5,64,32]{2,0,1:T(8,128)S(1)} %collective-permute-done.1), dimensions={2} | concatenate | bytes 2785280 | tf_op jit(solution)/shard_map/concatenate | solution.py:16
  124.5 0.2 fusion.20
  124.7 0.1 copy.8
  124.8 2.5 %collective-permute-start.3 = (f32[5,32,1088]{2,1,0:T(8,128)S(1)}, f32[5,32,1088]{2,1,0:T(8,128)S(1)}, u32[]{:S(2)}, u32[]{:S(2)}) collective-permute-start(f32[5,32,1088]{2,1,0:T(8,128)S(1)} %copy.8), channel_id=1, source_target_pairs={{1,0},{2,1},{3,2},{4,3},{5,4},{6,5},{7,6},{9,8},{10,9},{11,10},{12... | collective-permute-start | bytes 2088968 | tf_op jit(solution)/shard_map/ppermute | solution.py:20
  127.3 0.1 copy.7
  127.4 4.5 %collective-permute-start.2 = (f32[5,32,1088]{2,1,0:T(8,128)S(1)}, f32[5,32,1088]{2,1,0:T(8,128)S(1)}, u32[]{:S(2)}, u32[]{:S(2)}) collective-permute-start(f32[5,32,1088]{2,1,0:T(8,128)S(1)} %copy.7), channel_id=1, source_target_pairs={{0,1},{1,2},{2,3},{3,4},{4,5},{5,6},{6,7},{8,9},{9,10},{10,11},{11... | collective-permute-start | bytes 2088968 | tf_op jit(solution)/shard_map/ppermute | solution.py:18
  131.9 0.6 subtract_abs_fusion
  132.6 23.6 %collective-permute-done.3 = f32[5,32,1088]{2,1,0:T(8,128)S(1)} collective-permute-done((f32[5,32,1088]{2,1,0:T(8,128)S(1)}, f32[5,32,1088]{2,1,0:T(8,128)S(1)}, u32[]{:S(2)}, u32[]{:S(2)}) %collective-permute-start.3) | collective-permute-done | bytes 696352 | tf_op jit(solution)/shard_map/ppermute | solution.py:20
  156.2 0.5 copy.10
  156.6 6.0 %collective-permute-done.2 = f32[5,32,1088]{2,1,0:T(8,128)S(1)} collective-permute-done((f32[5,32,1088]{2,1,0:T(8,128)S(1)}, f32[5,32,1088]{2,1,0:T(8,128)S(1)}, u32[]{:S(2)}, u32[]{:S(2)}) %collective-permute-start.2) | collective-permute-done | bytes 696352 | tf_op jit(solution)/shard_map/ppermute | solution.py:18
  162.7 0.5 copy.9
  163.1 0.5 pad_maximum_fusion
  163.6 1.5 fusion.7
  165.1 9.0 %fusion.9 = f32[5,64,1024]{2,1,0:T(8,128)} fusion(f32[5,64,1088]{2,1,0:T(8,128)S(1)} %fusion.7, s32[1088,1024]{1,0:T(8,128)S(1)} %subtract_abs_fusion, s32[5]{0:T(128)S(1)} %copy-done, f32[5]{0:T(128)S(1)} %add_convert_fusion), kind=kOutput, calls=%fused_computation.11 | convolution fusion | flops 4284088320 | bytes 7159848 | tf_op jit(solution)/shard_map/kim,kmj->kij/dot_general | solution.py:50
  (5 shorter events, 0.0 us)
Async XLA Ops:
  6.5 108.2 %reduce-scatter.2.cloned.1.call-start = ((), (), s32[]{:S(2)}) async-start(), calls=%async_computation.1 | async-start | bytes 10485760 | tf_op jit(solution)/shard_map/reduce_scatter | solution.py:72
  43.1 75.7 %copy-start = (s32[5]{0:T(128)S(1)}, s32[5]{0:T(128)}, u32[]{:S(2)}) copy-start(s32[5]{0:T(128)} %param.7) | copy-start | bytes 64
  115.9 2.9 %collective-permute-start = (f32[5,64,32]{2,0,1:T(8,128)S(1)}, f32[5,64,32]{2,0,1:T(8,128)S(1)}, u32[]{:S(2)}, u32[]{:S(2)}) collective-permute-start(f32[5,64,32]{2,0,1:T(8,128)S(1)} %get-tuple-element.8), channel_id=1, source_target_pairs={{0,8},{8,16},{16,24},{1,9},{9,17},{17,25},{2,10},{10,18},{18,26},{... | collective-permute-start | bytes 122888 | tf_op jit(solution)/shard_map/ppermute | solution.py:18
  117.5 3.9 %collective-permute-start.1 = (f32[5,64,32]{2,0,1:T(8,128)S(1)}, f32[5,64,32]{2,0,1:T(8,128)S(1)}, u32[]{:S(2)}, u32[]{:S(2)}) collective-permute-start(f32[5,64,32]{2,0,1:T(8,128)S(1)} %get-tuple-element.7), channel_id=1, source_target_pairs={{8,0},{16,8},{24,16},{9,1},{17,9},{25,17},{10,2},{18,10},{26,18},{... | collective-permute-start | bytes 122888 | tf_op jit(solution)/shard_map/ppermute | solution.py:20
  124.8 31.3 %collective-permute-start.3 = (f32[5,32,1088]{2,1,0:T(8,128)S(1)}, f32[5,32,1088]{2,1,0:T(8,128)S(1)}, u32[]{:S(2)}, u32[]{:S(2)}) collective-permute-start(f32[5,32,1088]{2,1,0:T(8,128)S(1)} %copy.8), channel_id=1, source_target_pairs={{1,0},{2,1},{3,2},{4,3},{5,4},{6,5},{7,6},{9,8},{10,9},{11,10},{12... | collective-permute-start | bytes 2088968 | tf_op jit(solution)/shard_map/ppermute | solution.py:20
  127.4 35.2 %collective-permute-start.2 = (f32[5,32,1088]{2,1,0:T(8,128)S(1)}, f32[5,32,1088]{2,1,0:T(8,128)S(1)}, u32[]{:S(2)}, u32[]{:S(2)}) collective-permute-start(f32[5,32,1088]{2,1,0:T(8,128)S(1)} %copy.7), channel_id=1, source_target_pairs={{0,1},{1,2},{2,3},{3,4},{4,5},{5,6},{6,7},{8,9},{9,10},{10,11},{11... | collective-permute-start | bytes 2088968 | tf_op jit(solution)/shard_map/ppermute | solution.py:18
Sparse Core Ops, SparseCore 0:
  43.2 71.4 reduce-scatter.1
where the time goes:
time: 182 us; the launch traced here: 181 us
  waiting for transfers between devices  104 us (57%)
  matrix products  36.3 us (20%)
  between operations  13.5 us (7%)
  starting transfers between devices  9.81 us (5%)
  blocking collectives  7.5 us (4%)
  local copies, waits for them, and re-layouts  6.26 us (3%)
  other arithmetic  3.71 us (2%)
    reduce_scatter x1, waiting for transfers between devices, body(): shares = lax.psum_scatter(partials, 'chan', scatter_dimension=2, tiled=True)  71.6 us
    ppermute x2, waiting for transfers between devices, padded(): lax.ppermute(head, axis, [((i + 1) % count, i) for i in range(ends)])  26.2 us
    dot_general x1, matrix products, body(): jnp.dot(coefficients, flat, precision=lax.Precision.HIGHEST, preferred_el...  25.8 us
    dot_general x1, matrix products, column_pass(): jnp.einsum('kim,kmj->kij', extended, col_band, precision=lax.Precision.HI...  9 us
    psum x1, blocking collectives, body(): weight_total = lax.psum(jnp.sum(weight_floats), 'chan')  7.5 us
    ppermute x2, waiting for transfers between devices, padded(): lax.ppermute(tail, axis, [(i, (i + 1) % count) for i in range(ends)])  6.05 us
    ppermute x2, starting transfers between devices, padded(): lax.ppermute(tail, axis, [(i, (i + 1) % count) for i in range(ends)])  6.04 us
    ppermute x2, starting transfers between devices, padded(): lax.ppermute(head, axis, [((i + 1) % count, i) for i in range(ends)])  3.76 us
  transfers between devices with their start and end apart: 5, of which 4 were waited for; matrix products, arithmetic and copies ran while one was open for 1% of the time, Pallas kernels for 0%

commit v1 on v0

v1 whole, which is shorter than its diff:
```python
import jax
import jax.numpy as jnp
from jax import lax
from jax.experimental import pallas as pl
from jax.experimental.pallas import tpu as pltpu
from jax.sharding import PartitionSpec as P

MOMENTS = 5
HW_MAX = 32
LANES = 128
BLOCK = 256
TILE = 512
CHUNK = 16


def split(values):
    high = values.astype(jnp.bfloat16)
    low = (values - high.astype(jnp.float32)).astype(jnp.bfloat16)
    return high, low


def moments_kernel(place, weights, offsets, half_widths, images, give, own, total, cells, shots, arrivals, *, groups):
    chans, rows, cols = cells.shape
    owners = 2 * groups
    span = cols // owners
    first_row = pl.multiple_of(place[0], CHUNK)
    copies = [
        pltpu.make_async_copy(
            images.at[:, pl.ds(first_row, rows), pl.ds(part * span, span)],
            cells.at[:, :, pl.ds(part * span, span)],
            arrivals.at[part],
        )
        for part in range(owners)
    ]
    for copy in copies:
        copy.start()
    floats = [weights[chan].astype(jnp.float32) for chan in range(chans)]
    shifts = [offsets[chan] for chan in range(chans)]
    weight_sum = floats[0]
    for value in floats[1:]:
        weight_sum = weight_sum + value
    total[...] = jnp.full(total.shape, weight_sum, jnp.float32)
    edge = jnp.zeros((MOMENTS, rows, LANES), jnp.float32)
    shots[:, :, 0:LANES] = edge
    shots[:, :, LANES + cols : 2 * LANES + cols] = edge
    for part in range(owners):
        copies[part].wait()
        for row in range(0, rows, 8):

            def tile(step, carry):
                at = pl.multiple_of(part * span + step * TILE, TILE)
                sums = [jnp.zeros((8, TILE), jnp.float32)] * MOMENTS
                for chan in range(chans):
                    term = cells[chan, row : row + 8, pl.ds(at, TILE)] * floats[chan]
                    sums[0] = sums[0] + term
                    for power in range(1, MOMENTS):
                        term = term * shifts[chan]
                        sums[power] = sums[power] + term
                for power in range(MOMENTS):
                    shots[power, row : row + 8, pl.ds(LANES + at, TILE)] = sums[power]
                return carry

            lax.fori_loop(0, span // TILE, tile, 0)
    in_main = lax.broadcasted_iota(jnp.int32, (BLOCK, BLOCK), 0)
    out_main = lax.broadcasted_iota(jnp.int32, (BLOCK, BLOCK), 1)
    far_main = jnp.abs(in_main - out_main)
    in_edge = lax.broadcasted_iota(jnp.int32, (LANES, BLOCK), 0)
    in_edge = jnp.where(in_edge < LANES // 2, in_edge + BLOCK, in_edge - LANES)
    far_edge = jnp.abs(in_edge - lax.broadcasted_iota(jnp.int32, (LANES, BLOCK), 1))
    lane = lax.broadcasted_iota(jnp.int32, (rows, LANES), 1)
    for power in range(MOMENTS):
        reach = half_widths[power]
        main_band = (far_main <= reach).astype(jnp.float32).astype(jnp.bfloat16)
        edge_band = (far_edge <= reach).astype(jnp.float32).astype(jnp.bfloat16)
        mains, edges = [], []
        for slot in range(owners):
            start = pl.multiple_of(LANES + place[1 + slot] * span, LANES)
            for at in range(0, span, BLOCK):
                mains.append(shots[power, :, pl.ds(start + at, BLOCK)])
                left = shots[power, :, pl.ds(start + at - LANES, LANES)]
                right = shots[power, :, pl.ds(start + at + BLOCK, LANES)]
                edges.append(jnp.where(lane < LANES // 2, right, left))
        main_high, main_low = split(jnp.concatenate(mains, axis=0))
        edge_high, edge_low = split(jnp.concatenate(edges, axis=0))
        result = jnp.dot(main_high, main_band, preferred_element_type=jnp.float32)
        result = result + jnp.dot(main_low, main_band, preferred_element_type=jnp.float32)
        result = result + jnp.dot(
            jnp.concatenate([edge_high, edge_low], axis=1),
            jnp.concatenate([edge_band, edge_band], axis=0),
            preferred_element_type=jnp.float32,
        )
        count = 0
        for slot in range(owners):
            target = give if slot < groups else own
            for at in range(0, span, BLOCK):
                target[slot % groups, power, :, at : at + BLOCK] = result[count * rows : (count + 1) * rows]
                count += 1


def moments_of(place, chan_weights, freq_offsets, half_widths, beam_images, groups):
    chans, _, cols = beam_images.shape
    span = cols // (2 * groups)
    smem = pl.BlockSpec(memory_space=pltpu.SMEM)
    piece = jax.ShapeDtypeStruct((groups, MOMENTS, CHUNK, span), jnp.float32)
    return pl.pallas_call(
        lambda *refs: moments_kernel(*refs, groups=groups),
        in_specs=[smem, smem, smem, smem, pl.BlockSpec(memory_space=pl.ANY)],
        out_shape=(piece, piece, jax.ShapeDtypeStruct((8, LANES), jnp.float32)),
        scratch_shapes=[
            pltpu.VMEM((chans, CHUNK, cols), jnp.float32),
            pltpu.VMEM((MOMENTS, CHUNK, cols + 2 * LANES), jnp.float32),
            pltpu.SemaphoreType.DMA((2 * groups,)),
        ],
        cost_estimate=pl.CostEstimate(
            flops=20 * chans * CHUNK * cols, bytes_accessed=4 * chans * CHUNK * cols, transcendentals=0
        ),
        name="moments",
    )(place, chan_weights, freq_offsets, half_widths, beam_images)


def rows_kernel(place, half_widths, total, *refs):
    *pieces, out = refs
    rows = out.shape[1]
    depth = rows + 2 * HW_MAX
    out_row = lax.broadcasted_iota(jnp.int32, (rows, depth), 0) + HW_MAX
    stacked = lax.broadcasted_iota(jnp.int32, (rows, depth), 1)
    block = stacked // HW_MAX
    flipped = (depth // HW_MAX - 1 - block) * HW_MAX + (stacked - block * HW_MAX)
    distance = jnp.abs(jnp.where(place[0] == 0, stacked, flipped) - out_row)
    for power in range(MOMENTS):
        reach = half_widths[power]
        band = (distance <= reach).astype(jnp.float32).astype(jnp.bfloat16)
        high, low = split(jnp.concatenate([piece[power] for piece in pieces], axis=0))
        result = jnp.dot(
            jnp.concatenate([band, band], axis=1),
            jnp.concatenate([high, low], axis=0),
            preferred_element_type=jnp.float32,
        )
        divisor = total[...] * (2 * reach + 1).astype(jnp.float32)
        scale = (1.0 / divisor)[0:1, 0:1]
        out[power] = result * scale


def body(beam_images, chan_weights, freq_offsets, half_widths):
    _, slab_rows, all_cols = beam_images.shape
    chan_count = lax.axis_size("chan")
    slab_count = lax.axis_size("slab")
    groups = chan_count // 2
    span = all_cols // chan_count
    mine = lax.axis_index("chan")
    odd = lax.axis_index("slab") % 2
    group, core = mine // 2, mine % 2
    offsets = list(range(1, groups)) + [0]
    slots = [2 * ((group + step) % groups) + side for side in (1 - core, core) for step in offsets]
    swap = [(i, i ^ 1) for i in range(chan_count)]
    near = [(i, i ^ 1) for i in range(slab_count) if i ^ 1 < slab_count]
    far = [(i, ((i + 1) ^ 1) - 1) for i in range(1, slab_count) if ((i + 1) ^ 1) - 1 < slab_count]
    halves = {"far": odd * (slab_rows - HW_MAX), "near": (1 - odd) * (slab_rows - HW_MAX)}
    held, arrived = {"far": [], "near": []}, {"far": [], "near": []}
    for half in ("far", "near"):
        for at in range(0, HW_MAX, CHUNK):
            place = jnp.stack([halves[half] + at] + slots).astype(jnp.int32)
            give, own, total = moments_of(place, chan_weights, freq_offsets, half_widths, beam_images, groups)
            got = lax.ppermute(give, "chan", swap)
            kept = own[groups - 1] + got[groups - 1]
            for order, step in enumerate(offsets[:-1]):
                sent = own[order] + got[order]
                hop = [(i, (i + 2 * step) % chan_count) for i in range(chan_count)]
                kept = kept + lax.ppermute(sent, "chan", hop)
            held[half].append(kept)
            arrived[half].append(lax.ppermute(kept, "slab", far if half == "far" else near))
    total = total + lax.ppermute(total, "chan", swap)
    passed = total
    for step in offsets[:-1]:
        hop = [(i, (i + 2 * step) % chan_count) for i in range(chan_count)]
        total = total + lax.ppermute(passed, "chan", hop)
    pieces = arrived["far"] + held["far"] + held["near"] + arrived["near"]
    smem = pl.BlockSpec(memory_space=pltpu.SMEM)
    vmem = pl.BlockSpec(memory_space=pltpu.VMEM)
    return pl.pallas_call(
        rows_kernel,
        in_specs=[smem, smem, vmem] + [vmem] * len(pieces),
        out_specs=vmem,
        out_shape=jax.ShapeDtypeStruct((MOMENTS, slab_rows, span), jnp.float32),
        name="row_pass",
    )(odd.reshape(1).astype(jnp.int32), half_widths, total, *pieces)


def solution(mesh):
    placed = (P("chan", "slab", None), P("chan"), P("chan"), P())
    return jax.shard_map(
        body, mesh=mesh, in_specs=placed, out_specs=P(None, "slab", "chan"), check_vma=False
    )
```

time: 182 us -> 73.3 us (0.40)
  waiting for transfers between devices: 104 us -> 23.6 us
  matrix products: 36.3 us -> 0 us
  Pallas kernels: 0 us -> 24.9 us
  between operations: 13.5 us -> 0.22 us
  blocking collectives: 7.5 us -> 0 us
  starting transfers between devices: 9.81 us -> 15.1 us
  local copies, waits for them, and re-layouts: 6.26 us -> 3.28 us
  other arithmetic: 3.71 us -> 5.88 us
    reduce_scatter x1 -> x0, waiting for transfers between devices: 71.6 us -> none  [body(): shares = lax.psum_scatter(partials, 'chan', scatter_dimension=2, tiled=True)]
    dot_general x3 -> x0, matrix products: 36.3 us -> none  [the longest x1 25.8 us: body(): jnp.dot(coefficients, flat, precision=lax.Precision.HIGHEST, preferred_el...]
    pallas_call x0 -> x5, Pallas kernels: none -> 24.9 us  [the longest x4 21.5 us: moments_of(): pl.pallas_call(lambda *refs: moments_kernel(*refs, groups=groups), in_spe...]
    ppermute x4 -> x14, waiting for transfers between devices: 32.2 us -> 23.6 us  [the longest x4 17.6 us: body(): kept = kept + lax.ppermute(sent, 'chan', hop)]
    psum x1 -> x0, blocking collectives: 7.5 us -> none  [body(): weight_total = lax.psum(jnp.sum(weight_floats), 'chan')]
    add x0 -> x10, other arithmetic: none -> 5.88 us  [the longest x4 3.17 us: body(): kept = kept + lax.ppermute(sent, 'chan', hop)]
    ppermute x4 -> x14, starting transfers between devices: 9.81 us -> 15.1 us  [the longest x4 7.98 us: body(): lax.ppermute(kept, 'slab', far if half == 'far' else near)]
    concatenate x1 -> x0, local copies, waits for them, and re-layouts: 3.07 us -> none  [padded(): jnp.concatenate([lax.ppermute(tail, axis, [(i, (i + 1) % count) for i in...]
  transfers between devices with their start and end apart: 5 -> 14, of which waited for: 4 -> 7; matrix products, arithmetic and copies ran while one was open for 1% -> 11% of each run, Pallas kernels for 0% -> 22%
where the time goes in v1:
time: 73.3 us; the launch traced here: 73 us
  Pallas kernels  24.9 us (34%)
  waiting for transfers between devices  23.6 us (32%)
  starting transfers between devices  15.1 us (21%)
  other arithmetic  5.88 us (8%)
  local copies, waits for them, and re-layouts  3.28 us (4%)
    pallas_call x4, Pallas kernels, moments_of(): pl.pallas_call(lambda *refs: moments_kernel(*refs, groups=groups), in_spe...  21.5 us
    ppermute x4, waiting for transfers between devices, body(): kept = kept + lax.ppermute(sent, 'chan', hop)  17.6 us
    ppermute x4, starting transfers between devices, body(): lax.ppermute(kept, 'slab', far if half == 'far' else near)  7.98 us
    ppermute x4, starting transfers between devices, body(): kept = kept + lax.ppermute(sent, 'chan', hop)  4.31 us
    pallas_call x1, Pallas kernels, body(): pl.pallas_call(rows_kernel, in_specs=[smem, smem, vmem] + [vmem] * len(pi...  3.33 us
    add x4, other arithmetic, body(): kept = kept + lax.ppermute(sent, 'chan', hop)  3.17 us
    ppermute x4, waiting for transfers between devices, body(): lax.ppermute(kept, 'slab', far if half == 'far' else near)  2.67 us
    another operation x4, local copies, waits for them, and re-layouts, body(): place = jnp.stack([halves[half] + at] + slots).astype(jnp.int32)  2.57 us
  transfers between devices with their start and end apart: 14, of which 7 were waited for; matrix products, arithmetic and copies ran while one was open for 11% of the time, Pallas kernels for 22%

profile of v1, /device:TPU:12, one launch (start us, length us, event | category | flops | bytes accessed | tf_op | source)
XLA Modules:
  0.0 73.0 jit_solution(12468801289132255647)
XLA Ops:
  0.0 0.6 stack.53.refs_0_
  0.6 5.3 %moments.4 = (f32[2,5,16,1024]{3,2,1,0:T(8,128)}, f32[2,5,16,1024]{3,2,1,0:T(8,128)}, f32[8,128]{1,0:T(8,128)}) custom-call(s32[5]{0:T(128)} %stack.53.refs_0_, s32[16]{0:T(128)} %refs_1_.7, f32[16]{0:T(128)} %refs_2_.7, s32[5]{0:T(128)} %half_widths.1, f32[16,64,4096]{2,1,0:T(8,128)} %refs_4_.7), custom_call_target="tpu_custom_call" | custom-call | flops 20971520 | bytes 4194304 | tf_op jit(solution)/shard_map/moments/pallas_call | solution.py:105
  6.0 0.1 collective-permute-start.10
  6.1 0.7 stack.59.refs_0_
  6.7 5.3 %moments.7 = (f32[2,5,16,1024]{3,2,1,0:T(8,128)}, f32[2,5,16,1024]{3,2,1,0:T(8,128)}, f32[8,128]{1,0:T(8,128)}) custom-call(s32[5]{0:T(128)} %stack.59.refs_0_, s32[16]{0:T(128)} %refs_1_.7, f32[16]{0:T(128)} %refs_2_.7, s32[5]{0:T(128)} %half_widths.1, f32[16,64,4096]{2,1,0:T(8,128)} %refs_4_.7), custom_call_target="tpu_custom_call" | custom-call | flops 20971520 | bytes 4194304 | tf_op jit(solution)/shard_map/moments/pallas_call | solution.py:105
  12.1 0.6 collective-permute-start.8
  12.6 0.6 stack.57.refs_0_
  13.3 5.5 %moments.6 = (f32[2,5,16,1024]{3,2,1,0:T(8,128)}, f32[2,5,16,1024]{3,2,1,0:T(8,128)}, f32[8,128]{1,0:T(8,128)}) custom-call(s32[5]{0:T(128)} %stack.57.refs_0_, s32[16]{0:T(128)} %refs_1_.7, f32[16]{0:T(128)} %refs_2_.7, s32[5]{0:T(128)} %half_widths.1, f32[16,64,4096]{2,1,0:T(8,128)} %refs_4_.7), custom_call_target="tpu_custom_call" | custom-call | flops 20971520 | bytes 4194304 | tf_op jit(solution)/shard_map/moments/pallas_call | solution.py:105
  18.8 0.1 collective-permute-start.5
  18.9 0.7 stack.55.refs_0_
  19.5 5.3 %moments.5 = (f32[2,5,16,1024]{3,2,1,0:T(8,128)}, f32[2,5,16,1024]{3,2,1,0:T(8,128)}, f32[8,128]{1,0:T(8,128)}) custom-call(s32[5]{0:T(128)} %stack.55.refs_0_, s32[16]{0:T(128)} %refs_1_.7, f32[16]{0:T(128)} %refs_2_.7, s32[5]{0:T(128)} %half_widths.1, f32[16,64,4096]{2,1,0:T(8,128)} %refs_4_.7), custom_call_target="tpu_custom_call" | custom-call | flops 20971520 | bytes 4194304 | tf_op jit(solution)/shard_map/moments/pallas_call | solution.py:105
  24.9 0.6 collective-permute-start.2
  25.4 0.0 collective-permute-done.10
  25.5 1.6 %collective-permute-start.11 = (f32[5,16,1024]{2,1,0:T(8,128)S(1)}, f32[5,16,1024]{2,1,0:T(8,128)S(1)}, u32[]{:S(2)}, u32[]{:S(2)}) collective-permute-start(f32[5,16,1024]{2,1,0:T(8,128)S(1)} %fusion), channel_id=1, source_target_pairs={{0,16},{8,24},{16,0},{24,8},{1,17},{9,25},{17,1},{25,9},{2,18},{10... | collective-permute-start | bytes 983048 | tf_op jit(solution)/shard_map/ppermute | solution.py:169
  27.0 0.0 collective-permute-done.8
  27.0 1.0 %fusion.3 = f32[5,16,1024]{2,1,0:T(8,128)S(1)} fusion(f32[2,5,16,1024]{3,2,1,0:T(8,128)} %collective-permute-done.8, f32[2,5,16,1024]{3,2,1,0:T(8,128)S(1)} %copy-done.5), kind=kLoop, calls=%fused_computation.6 | loop fusion | flops 81920 | bytes 983040 | tf_op jit(solution)/shard_map/add | solution.py:167
  28.1 0.6 collective-permute-start.9
  28.7 0.0 collective-permute-done.5
  28.7 0.0 copy-done.6
  28.7 1.6 %collective-permute-start.6 = (f32[5,16,1024]{2,1,0:T(8,128)S(1)}, f32[5,16,1024]{2,1,0:T(8,128)S(1)}, u32[]{:S(2)}, u32[]{:S(2)}) collective-permute-start(f32[5,16,1024]{2,1,0:T(8,128)S(1)} %fusion.6), channel_id=1, source_target_pairs={{0,16},{8,24},{16,0},{24,8},{1,17},{9,25},{17,1},{25,9},{2,18},{10... | collective-permute-start | bytes 983048 | tf_op jit(solution)/shard_map/ppermute | solution.py:169
  30.3 0.0 collective-permute-done.2
  30.3 1.0 %fusion.9 = f32[5,16,1024]{2,1,0:T(8,128)S(1)} fusion(f32[2,5,16,1024]{3,2,1,0:T(8,128)S(1)} %collective-permute-done.2, f32[2,5,16,1024]{3,2,1,0:T(8,128)} %get-tuple-element.15), kind=kLoop, calls=%fused_computation.16 | loop fusion | flops 81920 | bytes 983040 | tf_op jit(solution)/shard_map/add | solution.py:167
  31.3 0.6 collective-permute-start.3
  31.9 4.2 %collective-permute-done.11 = f32[5,16,1024]{2,1,0:T(8,128)S(1)} collective-permute-done((f32[5,16,1024]{2,1,0:T(8,128)S(1)}, f32[5,16,1024]{2,1,0:T(8,128)S(1)}, u32[]{:S(2)}, u32[]{:S(2)}) %collective-permute-start.11) | collective-permute-done | bytes 327712 | tf_op jit(solution)/shard_map/ppermute | solution.py:169
  36.1 0.1 fusion.2.refs_5_
  36.2 0.6 collective-permute-start.13
  36.8 6.4 %collective-permute-done.9 = f32[5,16,1024]{2,1,0:T(8,128)S(1)} collective-permute-done((f32[5,16,1024]{2,1,0:T(8,128)S(1)}, f32[5,16,1024]{2,1,0:T(8,128)S(1)}, u32[]{:S(2)}, u32[]{:S(2)}) %collective-permute-start.9) | collective-permute-done | bytes 327712 | tf_op jit(solution)/shard_map/ppermute | solution.py:169
  43.1 1.0 %fusion.5.refs_4_ = f32[5,16,1024]{2,1,0:T(8,128)S(1)} fusion(f32[5,16,1024]{2,1,0:T(8,128)S(1)} %collective-permute-done.9, f32[2,5,16,1024]{3,2,1,0:T(8,128)} %collective-permute-done.8, f32[2,5,16,1024]{3,2,1,0:T(8,128)S(1)} %copy-done.5), kind=kLoop, calls=%fused_computation.9 | loop fusion | flops 163840 | bytes 1310720 | tf_op jit(solution)/shard_map/add | solution.py:169
  44.2 0.6 collective-permute-start.12
  44.8 5.4 %collective-permute-done.6 = f32[5,16,1024]{2,1,0:T(8,128)S(1)} collective-permute-done((f32[5,16,1024]{2,1,0:T(8,128)S(1)}, f32[5,16,1024]{2,1,0:T(8,128)S(1)}, u32[]{:S(2)}, u32[]{:S(2)}) %collective-permute-start.6) | collective-permute-done | bytes 327712 | tf_op jit(solution)/shard_map/ppermute | solution.py:169
  50.2 1.0 %fusion.8.refs_3_ = f32[5,16,1024]{2,1,0:T(8,128)S(1)} fusion(f32[5,16,1024]{2,1,0:T(8,128)S(1)} %collective-permute-done.6, f32[2,5,16,1024]{3,2,1,0:T(8,128)} %copy-done.7, f32[2,5,16,1024]{3,2,1,0:T(8,128)S(1)} %copy-done.6), kind=kLoop, calls=%fused_computation.14 | loop fusion | flops 163840 | bytes 1310720 | tf_op jit(solution)/shard_map/add | solution.py:169
  51.2 3.4 %collective-permute-start.7 = (f32[5,16,1024]{2,1,0:T(8,128)S(1)}, f32[5,16,1024]{2,1,0:T(8,128)S(1)}, u32[]{:S(2)}, u32[]{:S(2)}) collective-permute-start(f32[5,16,1024]{2,1,0:T(8,128)S(1)} %fusion.8.refs_3_), channel_id=1, source_target_pairs={{1,2},{2,1},{3,4},{4,3},{5,6},{6,5},{9,10},{10,9},{11,12},{12,11},... | collective-permute-start | bytes 983048 | tf_op jit(solution)/shard_map/ppermute | solution.py:171
  54.7 1.6 %collective-permute-done.3 = f32[5,16,1024]{2,1,0:T(8,128)S(1)} collective-permute-done((f32[5,16,1024]{2,1,0:T(8,128)S(1)}, f32[5,16,1024]{2,1,0:T(8,128)S(1)}, u32[]{:S(2)}, u32[]{:S(2)}) %collective-permute-start.3) | collective-permute-done | bytes 327712 | tf_op jit(solution)/shard_map/ppermute | solution.py:169
  56.3 1.0 %fusion.11.refs_2_ = f32[5,16,1024]{2,1,0:T(8,128)S(1)} fusion(f32[5,16,1024]{2,1,0:T(8,128)S(1)} %collective-permute-done.3, f32[2,5,16,1024]{3,2,1,0:T(8,128)S(1)} %collective-permute-done.2, f32[2,5,16,1024]{3,2,1,0:T(8,128)} %get-tuple-element.15), kind=kLoop, calls=%fused_computation.19 | loop fusion | flops 163840 | bytes 1310720 | tf_op jit(solution)/shard_map/add | solution.py:169
  57.3 3.4 %collective-permute-start.4 = (f32[5,16,1024]{2,1,0:T(8,128)S(1)}, f32[5,16,1024]{2,1,0:T(8,128)S(1)}, u32[]{:S(2)}, u32[]{:S(2)}) collective-permute-start(f32[5,16,1024]{2,1,0:T(8,128)S(1)} %fusion.11.refs_2_), channel_id=1, source_target_pairs={{1,2},{2,1},{3,4},{4,3},{5,6},{6,5},{9,10},{10,9},{11,12},{12,11},... | collective-permute-start | bytes 983048 | tf_op jit(solution)/shard_map/ppermute | solution.py:171
  60.7 0.0 copy-done.12
  60.8 0.1 collective-permute-start
  60.8 1.2 %collective-permute-done = f32[8,128]{1,0:T(8,128)S(1)} collective-permute-done((f32[8,128]{1,0:T(8,128)S(1)}, f32[8,128]{1,0:T(8,128)S(1)}, u32[]{:S(2)}, u32[]{:S(2)}) %collective-permute-start) | collective-permute-done | bytes 4128 | tf_op jit(solution)/shard_map/ppermute | solution.py:172
  62.0 1.5 %collective-permute-start.1 = (f32[8,128]{1,0:T(8,128)S(1)}, f32[8,128]{1,0:T(8,128)S(1)}, u32[]{:S(2)}, u32[]{:S(2)}) collective-permute-start(f32[8,128]{1,0:T(8,128)S(1)} %add.114), channel_id=1, source_target_pairs={{0,16},{8,24},{16,0},{24,8},{1,17},{9,25},{17,1},{25,9},{2,18},{10... | collective-permute-start | bytes 12296 | tf_op jit(solution)/shard_map/ppermute | solution.py:176
  63.5 2.1 %collective-permute-done.1 = f32[8,128]{1,0:T(8,128)S(1)} collective-permute-done((f32[8,128]{1,0:T(8,128)S(1)}, f32[8,128]{1,0:T(8,128)S(1)}, u32[]{:S(2)}, u32[]{:S(2)}) %collective-permute-start.1) | collective-permute-done | bytes 4128 | tf_op jit(solution)/shard_map/ppermute | solution.py:176
  65.6 0.6 add.115.total
  66.2 0.0 collective-permute-done.13.refs_7_
  66.2 0.0 collective-permute-done.12.refs_6_
  66.2 0.0 copy-start.9
  66.2 0.0 collective-permute-done.7.refs_1_
  66.2 2.7 %collective-permute-done.4.refs_0_ = f32[5,16,1024]{2,1,0:T(8,128)S(1)} collective-permute-done((f32[5,16,1024]{2,1,0:T(8,128)S(1)}, f32[5,16,1024]{2,1,0:T(8,128)S(1)}, u32[]{:S(2)}, u32[]{:S(2)}) %collective-permute-start.4) | collective-permute-done | bytes 327712 | tf_op jit(solution)/shard_map/ppermute | solution.py:171
  69.0 0.7 copy-done.11
  69.6 3.3 %row_pass.1 = f32[5,64,1024]{2,1,0:T(8,128)} custom-call(s32[1]{0:T(128)} %bitcast.place, s32[5]{0:T(128)} %half_widths.1, f32[8,128]{1,0:T(8,128)} %add.115.total, f32[5,16,1024]{2,1,0:T(8,128)} %copy-done.11, f32[5,16,1024]{2,1,0:T(8,128)} %copy-done.10, f32[5,16,1024]{2,1,0:T(8,128)} %copy-done.3, f32[5,16,1024]{2,1,0:T(8,128)} %copy-done.2, ...), custom_call_target="tpu_custom_call" | custom-call | tf_op jit(solution)/shard_map/row_pass/pallas_call | solution.py:180
  (25 shorter events, 0.1 us)
Async XLA Ops:
  6.0 19.5 %collective-permute-start.10 = (f32[2,5,16,1024]{3,2,1,0:T(8,128)}, f32[2,5,16,1024]{3,2,1,0:T(8,128)S(1)}, u32[]{:S(2)}, u32[]{:S(2)}) collective-permute-start(f32[2,5,16,1024]{3,2,1,0:T(8,128)} %get-tuple-element.22), channel_id=1, source_target_pairs={{0,8},{8,0},{16,24},{24,16},{1,9},{9,1},{17,25},{25,17},{2,10},{10... | collective-permute-start | bytes 1966088 | tf_op jit(solution)/shard_map/ppermute | solution.py:164
  12.1 15.0 %collective-permute-start.8 = (f32[2,5,16,1024]{3,2,1,0:T(8,128)}, f32[2,5,16,1024]{3,2,1,0:T(8,128)}, u32[]{:S(2)}, u32[]{:S(2)}) collective-permute-start(f32[2,5,16,1024]{3,2,1,0:T(8,128)} %get-tuple-element.20), channel_id=1, source_target_pairs={{0,8},{8,0},{16,24},{24,16},{1,9},{9,1},{17,25},{25,17},{2,10},{10... | collective-permute-start | bytes 1966088 | tf_op jit(solution)/shard_map/ppermute | solution.py:164
  13.3 12.2 %copy-start.4 = (f32[2,5,16,1024]{3,2,1,0:T(8,128)S(1)}, f32[2,5,16,1024]{3,2,1,0:T(8,128)}, u32[]{:S(2)}) copy-start(f32[2,5,16,1024]{3,2,1,0:T(8,128)} %get-tuple-element.21) | copy-start | bytes 1966084
  13.3 13.8 %copy-start.5 = (f32[2,5,16,1024]{3,2,1,0:T(8,128)S(1)}, f32[2,5,16,1024]{3,2,1,0:T(8,128)}, u32[]{:S(2)}) copy-start(f32[2,5,16,1024]{3,2,1,0:T(8,128)} %get-tuple-element.19) | copy-start | bytes 1966084
  18.8 9.9 %copy-start.6 = (f32[2,5,16,1024]{3,2,1,0:T(8,128)S(1)}, f32[2,5,16,1024]{3,2,1,0:T(8,128)}, u32[]{:S(2)}) copy-start(f32[2,5,16,1024]{3,2,1,0:T(8,128)} %get-tuple-element.17) | copy-start | bytes 1966084
  18.8 42.0 %copy-start.12 = (f32[8,128]{1,0:T(8,128)S(1)}, f32[8,128]{1,0:T(8,128)}, u32[]{:S(2)}) copy-start(f32[8,128]{1,0:T(8,128)} %get-tuple-element.14) | copy-start | bytes 12292
  18.8 9.9 %collective-permute-start.5 = (f32[2,5,16,1024]{3,2,1,0:T(8,128)}, f32[2,5,16,1024]{3,2,1,0:T(8,128)S(1)}, u32[]{:S(2)}, u32[]{:S(2)}) collective-permute-start(f32[2,5,16,1024]{3,2,1,0:T(8,128)} %get-tuple-element.18), channel_id=1, source_target_pairs={{0,8},{8,0},{16,24},{24,16},{1,9},{9,1},{17,25},{25,17},{2,10},{10... | collective-permute-start | bytes 1966088 | tf_op jit(solution)/shard_map/ppermute | solution.py:164
  24.9 5.4 %collective-permute-start.2 = (f32[2,5,16,1024]{3,2,1,0:T(8,128)}, f32[2,5,16,1024]{3,2,1,0:T(8,128)S(1)}, u32[]{:S(2)}, u32[]{:S(2)}) collective-permute-start(f32[2,5,16,1024]{3,2,1,0:T(8,128)} %get-tuple-element.16), channel_id=1, source_target_pairs={{0,8},{8,0},{16,24},{24,16},{1,9},{9,1},{17,25},{25,17},{2,10},{10... | collective-permute-start | bytes 1966088 | tf_op jit(solution)/shard_map/ppermute | solution.py:164
  25.5 10.6 %collective-permute-start.11 = (f32[5,16,1024]{2,1,0:T(8,128)S(1)}, f32[5,16,1024]{2,1,0:T(8,128)S(1)}, u32[]{:S(2)}, u32[]{:S(2)}) collective-permute-start(f32[5,16,1024]{2,1,0:T(8,128)S(1)} %fusion), channel_id=1, source_target_pairs={{0,16},{8,24},{16,0},{24,8},{1,17},{9,25},{17,1},{25,9},{2,18},{10... | collective-permute-start | bytes 983048 | tf_op jit(solution)/shard_map/ppermute | solution.py:169
  28.1 15.1 %collective-permute-start.9 = (f32[5,16,1024]{2,1,0:T(8,128)S(1)}, f32[5,16,1024]{2,1,0:T(8,128)S(1)}, u32[]{:S(2)}, u32[]{:S(2)}) collective-permute-start(f32[5,16,1024]{2,1,0:T(8,128)S(1)} %fusion.3), channel_id=1, source_target_pairs={{0,16},{8,24},{16,0},{24,8},{1,17},{9,25},{17,1},{25,9},{2,18},{10... | collective-permute-start | bytes 983048 | tf_op jit(solution)/shard_map/ppermute | solution.py:169
  28.7 3.2 %copy-start.7 = (f32[2,5,16,1024]{3,2,1,0:T(8,128)}, f32[2,5,16,1024]{3,2,1,0:T(8,128)S(1)}, u32[]{:S(2)}) copy-start(f32[2,5,16,1024]{3,2,1,0:T(8,128)S(1)} %collective-permute-done.5) | copy-start | bytes 1966084
  28.7 21.5 %collective-permute-start.6 = (f32[5,16,1024]{2,1,0:T(8,128)S(1)}, f32[5,16,1024]{2,1,0:T(8,128)S(1)}, u32[]{:S(2)}, u32[]{:S(2)}) collective-permute-start(f32[5,16,1024]{2,1,0:T(8,128)S(1)} %fusion.6), channel_id=1, source_target_pairs={{0,16},{8,24},{16,0},{24,8},{1,17},{9,25},{17,1},{25,9},{2,18},{10... | collective-permute-start | bytes 983048 | tf_op jit(solution)/shard_map/ppermute | solution.py:169
  31.3 25.0 %collective-permute-start.3 = (f32[5,16,1024]{2,1,0:T(8,128)S(1)}, f32[5,16,1024]{2,1,0:T(8,128)S(1)}, u32[]{:S(2)}, u32[]{:S(2)}) collective-permute-start(f32[5,16,1024]{2,1,0:T(8,128)S(1)} %fusion.9), channel_id=1, source_target_pairs={{0,16},{8,24},{16,0},{24,8},{1,17},{9,25},{17,1},{25,9},{2,18},{10... | collective-permute-start | bytes 983048 | tf_op jit(solution)/shard_map/ppermute | solution.py:169
  36.2 32.7 %copy-start = (f32[5,16,1024]{2,1,0:T(8,128)}, f32[5,16,1024]{2,1,0:T(8,128)S(1)}, u32[]{:S(2)}) copy-start(f32[5,16,1024]{2,1,0:T(8,128)S(1)} %fusion.2.refs_5_) | copy-start | bytes 983044
  36.2 30.0 %collective-permute-start.13 = (f32[5,16,1024]{2,1,0:T(8,128)S(1)}, f32[5,16,1024]{2,1,0:T(8,128)S(1)}, u32[]{:S(2)}, u32[]{:S(2)}) collective-permute-start(f32[5,16,1024]{2,1,0:T(8,128)S(1)} %fusion.2.refs_5_), channel_id=1, source_target_pairs={{0,1},{1,0},{2,3},{3,2},{4,5},{5,4},{6,7},{7,6},{8,9},{9,8},{10,11... | collective-permute-start | bytes 983048 | tf_op jit(solution)/shard_map/ppermute | solution.py:171
  44.2 24.7 %copy-start.1 = (f32[5,16,1024]{2,1,0:T(8,128)}, f32[5,16,1024]{2,1,0:T(8,128)S(1)}, u32[]{:S(2)}) copy-start(f32[5,16,1024]{2,1,0:T(8,128)S(1)} %fusion.5.refs_4_) | copy-start | bytes 983044
  44.2 22.0 %collective-permute-start.12 = (f32[5,16,1024]{2,1,0:T(8,128)S(1)}, f32[5,16,1024]{2,1,0:T(8,128)S(1)}, u32[]{:S(2)}, u32[]{:S(2)}) collective-permute-start(f32[5,16,1024]{2,1,0:T(8,128)S(1)} %fusion.5.refs_4_), channel_id=1, source_target_pairs={{0,1},{1,0},{2,3},{3,2},{4,5},{5,4},{6,7},{7,6},{8,9},{9,8},{10,11... | collective-permute-start | bytes 983048 | tf_op jit(solution)/shard_map/ppermute | solution.py:171
  51.2 17.7 %copy-start.2 = (f32[5,16,1024]{2,1,0:T(8,128)}, f32[5,16,1024]{2,1,0:T(8,128)S(1)}, u32[]{:S(2)}) copy-start(f32[5,16,1024]{2,1,0:T(8,128)S(1)} %fusion.8.refs_3_) | copy-start | bytes 983044
  51.2 15.0 %collective-permute-start.7 = (f32[5,16,1024]{2,1,0:T(8,128)S(1)}, f32[5,16,1024]{2,1,0:T(8,128)S(1)}, u32[]{:S(2)}, u32[]{:S(2)}) collective-permute-start(f32[5,16,1024]{2,1,0:T(8,128)S(1)} %fusion.8.refs_3_), channel_id=1, source_target_pairs={{1,2},{2,1},{3,4},{4,3},{5,6},{6,5},{9,10},{10,9},{11,12},{12,11},... | collective-permute-start | bytes 983048 | tf_op jit(solution)/shard_map/ppermute | solution.py:171
  57.3 11.6 %copy-start.3 = (f32[5,16,1024]{2,1,0:T(8,128)}, f32[5,16,1024]{2,1,0:T(8,128)S(1)}, u32[]{:S(2)}) copy-start(f32[5,16,1024]{2,1,0:T(8,128)S(1)} %fusion.11.refs_2_) | copy-start | bytes 983044
  57.3 11.6 %collective-permute-start.4 = (f32[5,16,1024]{2,1,0:T(8,128)S(1)}, f32[5,16,1024]{2,1,0:T(8,128)S(1)}, u32[]{:S(2)}, u32[]{:S(2)}) collective-permute-start(f32[5,16,1024]{2,1,0:T(8,128)S(1)} %fusion.11.refs_2_), channel_id=1, source_target_pairs={{1,2},{2,1},{3,4},{4,3},{5,6},{6,5},{9,10},{10,9},{11,12},{12,11},... | collective-permute-start | bytes 983048 | tf_op jit(solution)/shard_map/ppermute | solution.py:171
  60.8 1.2 %collective-permute-start = (f32[8,128]{1,0:T(8,128)S(1)}, f32[8,128]{1,0:T(8,128)S(1)}, u32[]{:S(2)}, u32[]{:S(2)}) collective-permute-start(f32[8,128]{1,0:T(8,128)S(1)} %copy-done.12), channel_id=1, source_target_pairs={{0,8},{8,0},{16,24},{24,16},{1,9},{9,1},{17,25},{25,17},{2,10},{10... | collective-permute-start | bytes 12296 | tf_op jit(solution)/shard_map/ppermute | solution.py:172
  62.0 3.6 %collective-permute-start.1 = (f32[8,128]{1,0:T(8,128)S(1)}, f32[8,128]{1,0:T(8,128)S(1)}, u32[]{:S(2)}, u32[]{:S(2)}) collective-permute-start(f32[8,128]{1,0:T(8,128)S(1)} %add.114), channel_id=1, source_target_pairs={{0,16},{8,24},{16,0},{24,8},{1,17},{9,25},{17,1},{25,9},{2,18},{10... | collective-permute-start | bytes 12296 | tf_op jit(solution)/shard_map/ppermute | solution.py:176
  66.2 2.7 %copy-start.8 = (f32[5,16,1024]{2,1,0:T(8,128)}, f32[5,16,1024]{2,1,0:T(8,128)S(1)}, u32[]{:S(2)}) copy-start(f32[5,16,1024]{2,1,0:T(8,128)S(1)} %collective-permute-done.13.refs_7_) | copy-start | bytes 983044
  66.2 2.7 %copy-start.9 = (f32[5,16,1024]{2,1,0:T(8,128)}, f32[5,16,1024]{2,1,0:T(8,128)S(1)}, u32[]{:S(2)}) copy-start(f32[5,16,1024]{2,1,0:T(8,128)S(1)} %collective-permute-done.12.refs_6_) | copy-start | bytes 983044
  66.2 2.7 %copy-start.10 = (f32[5,16,1024]{2,1,0:T(8,128)}, f32[5,16,1024]{2,1,0:T(8,128)S(1)}, u32[]{:S(2)}) copy-start(f32[5,16,1024]{2,1,0:T(8,128)S(1)} %collective-permute-done.7.refs_1_) | copy-start | bytes 983044
  68.9 0.7 copy-start.11

commit v2 on v0

v2 whole, which is shorter than its diff:
```python
import jax
import jax.numpy as jnp
from jax import lax
from jax.experimental import pallas as pl
from jax.experimental.pallas import tpu as pltpu
from jax.sharding import PartitionSpec as P


MOMENTS = 5
LANES = 128
BLOCK = 256
ROWS = 8
PARTS = 2

CALLS = (((('far', 0), ('far', 8)), ((0, 2, 0, 5),)), ((('near', 0), ('near', 8)), ((0, 2, 0, 5),)), ((('near', 16), ('near', 24)), ((0, 2, 0, 5),)), ((('far', 16), ('far', 24)), ((0, 2, 0, 4), (0, 2, 4, 5))))


def steps_of(groups):
    return list(range(1, groups)) + [0]


def split(values):
    high = values.astype(jnp.bfloat16)
    low = (values - high.astype(jnp.float32)).astype(jnp.bfloat16)
    return high, low


def moments_kernel(sources, images, *refs, bands, pieces):
    outs, shots = refs[: -4 - len(bands)], refs[-len(bands) :]
    values, cells, bars, arrivals = refs[-4 - len(bands) : -len(bands)]
    _, chans, rows, cols = cells.shape
    groups = outs[0].shape[0] + 1
    owners = 2 * groups
    span = cols // owners
    wide = cols // PARTS
    mine = lax.axis_index("chan")
    odd = lax.axis_index("slab") % 2
    copies = []
    for band, (half, at) in enumerate(bands):
        below = odd if half == "far" else 1 - odd
        first_row = pl.multiple_of(jnp.where(below == 1, images.shape[1] - ROWS - at, at), ROWS)
        for lane_at in range(0, cols, wide):
            copies.append(
                pltpu.make_async_copy(
                    images.at[:, pl.ds(first_row, rows), pl.ds(lane_at, wide)],
                    cells.at[band, :, :, pl.ds(lane_at, wide)],
                    arrivals.at[len(copies)],
                )
            )
    for copy in copies:
        copy.start()
    load = pltpu.make_async_copy(sources, values, arrivals.at[len(copies)])
    load.start()
    load.wait()
    group, core = mine // 2, mine % 2
    slots = [
        2 * ((group + step) % groups) + side for side in (1 - core, core) for step in steps_of(groups)
    ]
    if len(outs) > 4 * len(pieces):
        weight_sum = values[0]
        for chan in range(1, chans):
            weight_sum = weight_sum + values[chan]
        outs[-1][...] = jnp.full(outs[-1].shape, weight_sum, jnp.float32)
    edge = jnp.zeros((MOMENTS, rows, LANES), jnp.float32)
    for shot in shots:
        shot[:, :, 0:LANES] = edge
        shot[:, :, LANES + cols : 2 * LANES + cols] = edge
    depth = rows * chans
    row_at = lax.broadcasted_iota(jnp.int32, (rows, depth), 0)
    col_at = lax.broadcasted_iota(jnp.int32, (rows, depth), 1)
    same_row = col_at % rows == row_at
    weight = jnp.zeros((rows, depth), jnp.float32)
    shift = jnp.zeros((rows, depth), jnp.float32)
    for chan in range(chans):
        here = same_row & (col_at // rows == chan)
        weight = jnp.where(here, values[chan], weight)
        shift = jnp.where(here, values[chans + chan], shift)
    terms = [weight]
    for _ in range(1, MOMENTS):
        terms.append(terms[-1] * shift)
    high, low = split(jnp.concatenate(terms, axis=0))
    mixer = jnp.concatenate(
        [
            jnp.concatenate([high, high], axis=1).astype(jnp.float32),
            jnp.concatenate([low, jnp.zeros_like(low)], axis=1).astype(jnp.float32),
        ],
        axis=0,
    ).astype(jnp.bfloat16)
    in_at = lax.broadcasted_iota(jnp.int32, (BLOCK + LANES, BLOCK), 0)
    in_at = jnp.where(
        in_at < BLOCK + LANES // 2, in_at, jnp.where(in_at < BLOCK, in_at, in_at - BLOCK - LANES)
    )
    distance = jnp.abs(in_at - lax.broadcasted_iota(jnp.int32, (BLOCK + LANES, BLOCK), 1))
    for power in range(MOMENTS):
        reach = values[2 * chans + power].astype(jnp.int32)
        bars[power] = (distance <= reach).astype(jnp.float32).astype(jnp.bfloat16)
    lane = lax.broadcasted_iota(jnp.int32, (rows, LANES), 1)

    def mix(band, lane_at):
        stack = cells[band, :, :, lane_at : lane_at + BLOCK].reshape(depth, BLOCK)
        mixed = jnp.dot(mixer, jnp.concatenate(split(stack), axis=0), preferred_element_type=jnp.float32)
        mixed = mixed[: rows * MOMENTS] + mixed[rows * MOMENTS :]
        shots[band][:, :, LANES + lane_at : LANES + lane_at + BLOCK] = mixed.reshape(MOMENTS, rows, BLOCK)

    def smooth(band, power):
        mains, edges = [], []
        for slot in range(owners):
            start = pl.multiple_of(LANES + slots[slot] * span, LANES)
            for lane_at in range(0, span, BLOCK):
                mains.append(shots[band][power, :, pl.ds(start + lane_at, BLOCK)])
                left = shots[band][power, :, pl.ds(start + lane_at - LANES, LANES)]
                right = shots[band][power, :, pl.ds(start + lane_at + BLOCK, LANES)]
                edges.append(jnp.where(lane < LANES // 2, right, left))
        main_high, main_low = split(jnp.concatenate(mains, axis=0))
        edge_high, edge_low = split(jnp.concatenate(edges, axis=0))
        main_bar, edge_bar = bars[power, :BLOCK], bars[power, BLOCK:]
        result = jnp.dot(main_high, main_bar, preferred_element_type=jnp.float32)
        result = result + jnp.dot(main_low, main_bar, preferred_element_type=jnp.float32)
        result = result + jnp.dot(
            jnp.concatenate([edge_high, edge_low], axis=1),
            jnp.concatenate([edge_bar, edge_bar], axis=0),
            preferred_element_type=jnp.float32,
        )
        result = result.reshape(owners, span // BLOCK, rows, BLOCK)
        for index, (first, size, low_power, high_power) in enumerate(pieces):
            if not (first <= band < first + size and low_power <= power < high_power):
                continue
            row = (band - first) * rows
            for slot in range(owners):
                order = slot % groups
                target = outs[4 * index + 2 * (slot >= groups) + (order == groups - 1)]
                for block in range(span // BLOCK):
                    target[
                        order % (groups - 1),
                        power - low_power,
                        row : row + rows,
                        block * BLOCK : (block + 1) * BLOCK,
                    ] = result[slot, block]

    for band in range(len(bands)):
        ready = [(band - 1, power) for power in range(MOMENTS)] if band > 0 else []
        for part in range(PARTS):
            copies[PARTS * band + part].wait()
            work = [(part * wide + at) for at in range(0, wide, BLOCK)]
            share = ready[part * MOMENTS // PARTS : (part + 1) * MOMENTS // PARTS]
            for index, lane_at in enumerate(work):
                mix(band, lane_at)
                if index % 2 == 1 and share:
                    smooth(*share.pop(0))
            for item in share:
                smooth(*item)
    for power in range(MOMENTS):
        smooth(len(bands) - 1, power)


def moments_of(values, beam_images, groups, bands, pieces, weigh):
    chans, _, cols = beam_images.shape
    span = cols // (2 * groups)
    outs = []
    for _, size, low_power, high_power in pieces:
        for count in (groups - 1, 1) * 2:
            shape = (count, high_power - low_power, size * ROWS, span)
            outs.append(jax.ShapeDtypeStruct(shape, jnp.float32))
    if weigh:
        outs.append(jax.ShapeDtypeStruct((8, LANES), jnp.float32))
    work = len(bands) * ROWS * chans * cols
    return pl.pallas_call(
        lambda *refs: moments_kernel(*refs, bands=bands, pieces=pieces),
        in_specs=[pl.BlockSpec(memory_space=pl.ANY), pl.BlockSpec(memory_space=pl.ANY)],
        out_shape=tuple(outs),
        scratch_shapes=[
            pltpu.SMEM(values.shape, jnp.float32),
            pltpu.VMEM((len(bands), chans, ROWS, cols), jnp.float32),
            pltpu.VMEM((MOMENTS, BLOCK + LANES, BLOCK), jnp.bfloat16),
            pltpu.SemaphoreType.DMA((PARTS * len(bands) + 1,)),
            *[pltpu.VMEM((MOMENTS, ROWS, cols + 2 * LANES), jnp.float32) for _ in bands],
        ],
        cost_estimate=pl.CostEstimate(flops=20 * work, bytes_accessed=4 * work, transcendentals=0),
        compiler_params=pltpu.CompilerParams(vmem_limit_bytes=48 * 2**20),
        name="moments",
    )(values, beam_images)


def window(shape, groups, first_row, slab_rows, odd):
    out_row = lax.broadcasted_iota(jnp.int32, shape, 0) + first_row
    stacked = lax.broadcasted_iota(jnp.int32, shape, 1)
    place = jnp.zeros(shape, jnp.int32)
    for index, (half, at, mine) in enumerate(groups):
        below = odd if half == "far" else 1 - odd
        lower = slab_rows - ROWS - at if mine else slab_rows + at
        upper = at if mine else -ROWS - at
        start = jnp.where(below == 1, lower, upper) - index * ROWS
        place = jnp.where(stacked // ROWS == index, stacked + start, place)
    return jnp.abs(place - out_row)


def banded(distance, reach, rows):
    bar = (distance <= reach).astype(jnp.float32).astype(jnp.bfloat16)
    high, low = split(rows)
    return jnp.dot(bar, high, preferred_element_type=jnp.float32) + jnp.dot(
        bar, low, preferred_element_type=jnp.float32
    )


def scale_of(total, reach):
    return (1.0 / (total[...] * (2 * reach + 1).astype(jnp.float32)))[0:1, 0:1]


def inner_kernel(values, total, *refs, chans, groups, half, bounds):
    *pieces, out, rest = refs
    odd = lax.axis_index("slab") % 2
    below = odd if half == "far" else 1 - odd
    rows, late = out.shape[1], rest.shape[1]
    distance = window((rows, ROWS * len(groups)), groups, 0, rows, odd)
    for power in range(MOMENTS):
        reach = values[2 * chans + power].astype(jnp.int32)
        parts = [
            piece[power - low]
            for piece, low in zip(pieces, bounds)
            if low <= power < low + piece.shape[0]
        ]
        result = banded(distance, reach, jnp.concatenate(parts, axis=0))
        out[power] = result * scale_of(total, reach)
        rest[power] = jnp.where(below == 1, result[rows - late :], result[:late])


def edge_kernel(values, total, rest, *refs, chans, groups, starts):
    *lasts, _, out, edge, sent = refs
    odd = lax.axis_index("slab") % 2
    slab_rows, late = out.shape[1], rest.shape[1]
    below = odd if groups[0][0] == "far" else 1 - odd
    first_row = pl.multiple_of(jnp.where(below == 1, slab_rows - late, 0), ROWS)
    distance = window((late, ROWS * len(groups)), groups, first_row, slab_rows, odd)
    copies = []
    for power in range(MOMENTS):
        reach = values[2 * chans + power].astype(jnp.int32)
        index = max(index for index, start in enumerate(starts) if start <= power)
        last = lasts[index][power - starts[index]]
        edge[power] = (rest[power] + banded(distance, reach, last)) * scale_of(total, reach)
        copies.append(
            pltpu.make_async_copy(edge.at[power], out.at[power, pl.ds(first_row, late), :], sent.at[power])
        )
        copies[-1].start()
    for copy in copies:
        copy.wait()


def body(beam_images, chan_weights, freq_offsets, half_widths):
    chans, slab_rows, all_cols = beam_images.shape
    chan_count = lax.axis_size("chan")
    slab_count = lax.axis_size("slab")
    groups = chan_count // 2
    span = all_cols // chan_count
    extent = 2 * chans + MOMENTS
    slot = jnp.arange(extent)
    spread = [
        jnp.pad(part, (before, extent - before - part.shape[0]))
        for part, before in ((chan_weights, 0), (half_widths, 2 * chans), (freq_offsets, chans))
    ]
    values = jnp.where(slot // chans == 1, spread[2], (spread[0] + spread[1]).astype(jnp.float32))
    steps = steps_of(groups)
    hops = [[(i, (i + 2 * step) % chan_count) for i in range(chan_count)] for step in steps[:-1]]
    swap = [(i, i ^ 1) for i in range(chan_count)]
    pairs = {
        "near": [(i, i ^ 1) for i in range(slab_count) if i ^ 1 < slab_count],
        "far": [(i, ((i + 1) ^ 1) - 1) for i in range(1, slab_count) if ((i + 1) ^ 1) - 1 < slab_count],
    }
    held, arrived, covers = [], [], []
    for call, (bands, pieces) in enumerate(CALLS):
        outs = moments_of(values, beam_images, groups, bands, pieces, call == len(CALLS) - 1)
        for index, (first, size, low, high) in enumerate(pieces):
            give, give_kept, own, own_kept = outs[4 * index : 4 * index + 4]
            got = lax.ppermute(give, "chan", swap)
            got_kept = lax.ppermute(give_kept, "chan", swap)
            kept = own_kept[0] + got_kept[0]
            for order, hop in enumerate(hops):
                sent = own[order] + got[order]
                came = lax.ppermute(sent, "chan", hop)
                kept = kept + came
            held.append(kept)
            half = bands[first][0]
            covers.append((bands[first : first + size], low))
            arrived.append(lax.ppermute(kept, "slab", pairs[half]))
    total = outs[-1]
    total = total + lax.ppermute(total, "chan", swap)
    passed = total
    for hop in hops:
        total = total + lax.ppermute(passed, "chan", hop)
    smem = pl.BlockSpec(memory_space=pltpu.SMEM)
    vmem = pl.BlockSpec(memory_space=pltpu.VMEM)
    anywhere = pl.BlockSpec(memory_space=pl.ANY)
    last = len(CALLS[-1][1])
    pieces = held + arrived[:-last]
    groups = [(*band, True, low) for cover, low in covers for band in cover]
    groups += [(*band, False, low) for cover, low in covers[:-last] for band in cover]
    groups = [group[:3] for group in groups if group[3] == 0]
    bounds = [low for _, low in covers] + [low for _, low in covers[:-last]]
    starts = [low for _, low in covers[-last:]]
    edges = covers[-1][0]
    late = len(edges) * ROWS
    shape = jax.ShapeDtypeStruct((MOMENTS, slab_rows, span), jnp.float32)
    result, rest = pl.pallas_call(
        lambda *refs: inner_kernel(
            *refs, chans=chans, groups=groups, half=edges[0][0], bounds=bounds
        ),
        in_specs=[smem, vmem] + [vmem] * len(pieces),
        out_specs=(vmem, vmem),
        out_shape=(shape, jax.ShapeDtypeStruct((MOMENTS, late, span), jnp.float32)),
        compiler_params=pltpu.CompilerParams(vmem_limit_bytes=16 * 2**20),
        name="inner_rows",
    )(values, total, *pieces)
    return pl.pallas_call(
        lambda *refs: edge_kernel(
            *refs, chans=chans, groups=[(*band, False) for band in edges], starts=starts
        ),
        in_specs=[smem, vmem, vmem] + [vmem] * last + [anywhere],
        out_specs=anywhere,
        out_shape=shape,
        scratch_shapes=[
            pltpu.VMEM((MOMENTS, late, span), jnp.float32),
            pltpu.SemaphoreType.DMA((MOMENTS,)),
        ],
        input_output_aliases={3 + last: 0},
        compiler_params=pltpu.CompilerParams(vmem_limit_bytes=16 * 2**20),
        name="edge_rows",
    )(values, total, rest, *arrived[-last:], result)


def solution(mesh):
    placed = (P("chan", "slab", None), P("chan"), P("chan"), P())

    return jax.shard_map(body, mesh=mesh, in_specs=placed, out_specs=P(None, "slab", "chan"), check_vma=False)
```

time: 182 us -> 76.1 us (0.42)
  waiting for transfers between devices: 104 us -> 34.7 us
  matrix products: 36.3 us -> 0 us
  Pallas kernels: 0 us -> 16.9 us
  between operations: 13.5 us -> 0.2 us
  starting transfers between devices: 9.81 us -> 22.4 us
  blocking collectives: 7.5 us -> 0 us
  local copies, waits for them, and re-layouts: 6.26 us -> 0 us
  other arithmetic: 3.71 us -> 1.2 us
    reduce_scatter x1 -> x0, waiting for transfers between devices: 71.6 us -> none  [body(): shares = lax.psum_scatter(partials, 'chan', scatter_dimension=2, tiled=True)]
    dot_general x3 -> x0, matrix products: 36.3 us -> none  [the longest x1 25.8 us: body(): jnp.dot(coefficients, flat, precision=lax.Precision.HIGHEST, preferred_el...]
    pallas_call x0 -> x6, Pallas kernels: none -> 16.9 us  [the longest x4 13.2 us: moments_of(): pl.pallas_call(lambda *refs: moments_kernel(*refs, bands=bands, pieces=pi...]
    ppermute x4 -> x22, starting transfers between devices: 9.81 us -> 22.4 us  [the longest x5 12.2 us: body(): arrived.append(lax.ppermute(kept, 'slab', pairs[half]))]
    psum x1 -> x0, blocking collectives: 7.5 us -> none  [body(): weight_total = lax.psum(jnp.sum(weight_floats), 'chan')]
    concatenate x1 -> x0, local copies, waits for them, and re-layouts: 3.07 us -> none  [padded(): jnp.concatenate([lax.ppermute(tail, axis, [(i, (i + 1) % count) for i in...]
    ppermute x4 -> x22, waiting for transfers between devices: 32.2 us -> 34.7 us  [the longest x5 21.6 us: body(): came = lax.ppermute(sent, 'chan', hop)]
  transfers between devices with their start and end apart: 5 -> 22, of which waited for: 4 -> 7; matrix products, arithmetic and copies ran while one was open for 1% -> 1% of each run, Pallas kernels for 0% -> 16%
where the time goes in v2:
time: 76.1 us; the launch traced here: 75.4 us
  waiting for transfers between devices  34.7 us (46%)
  starting transfers between devices  22.4 us (29%)
  Pallas kernels  16.9 us (22%)
  other arithmetic  1.2 us (2%)
    ppermute x5, waiting for transfers between devices, body(): came = lax.ppermute(sent, 'chan', hop)  21.6 us
    pallas_call x4, Pallas kernels, moments_of(): pl.pallas_call(lambda *refs: moments_kernel(*refs, bands=bands, pieces=pi...  13.2 us
    ppermute x5, starting transfers between devices, body(): arrived.append(lax.ppermute(kept, 'slab', pairs[half]))  12.2 us
    ppermute x5, waiting for transfers between devices, body(): arrived.append(lax.ppermute(kept, 'slab', pairs[half]))  12.2 us
    ppermute x5, starting transfers between devices, body(): came = lax.ppermute(sent, 'chan', hop)  5.96 us
    pallas_call x1, Pallas kernels, body(): pl.pallas_call(lambda *refs: inner_kernel(*refs, chans=chans, groups=grou...  2.19 us
    ppermute x5, starting transfers between devices, body(): got_kept = lax.ppermute(give_kept, 'chan', swap)  1.63 us
    ppermute x1, starting transfers between devices, body(): total = total + lax.ppermute(passed, 'chan', hop)  1.56 us
  transfers between devices with their start and end apart: 22, of which 7 were waited for; matrix products, arithmetic and copies ran while one was open for 1% of the time, Pallas kernels for 16%

profile of v2, /device:TPU:12, one launch (start us, length us, event | category | flops | bytes accessed | tf_op | source)
XLA Modules:
  0.0 75.4 jit_solution(187609223237466293)
XLA Ops:
  0.0 0.8 %compare_select_fusion.refs_0_ = f32[37]{0:T(128)S(1)} fusion(s32[5]{0:T(128)} %param.7, s32[16]{0:T(128)} %param.5, f32[16]{0:T(128)} %param.6), kind=kLoop, calls=%fused_computation.10 | loop fusion | flops 444 | bytes 296 | tf_op jit(solution)/shard_map/jit(_where)/select_n | solution.py:260
  0.8 3.3 %moments.4 = (f32[1,4,16,1024]{3,2,1,0:T(8,128)S(1)}, f32[1,4,16,1024]{3,2,1,0:T(8,128)S(1)}, f32[1,4,16,1024]{3,2,1,0:T(8,128)S(1)}, f32[1,4,16,1024]{3,2,1,0:T...) custom-call(f32[37]{0:T(128)S(1)} %compare_select_fusion.refs_0_, ...), custom_call_target="tpu_custom_call" | custom-call | flops 20971520 | bytes 4194304 | tf_op jit(solution)/shard_map/moments/pallas_call | solution.py:167
  4.1 0.1 collective-permute-start.15
  4.2 0.5 collective-permute-start.12
  4.7 0.1 collective-permute-start
  4.7 0.4 collective-permute-start.11
  5.2 3.3 %moments.6 = (f32[1,5,16,1024]{3,2,1,0:T(8,128)S(1)}, f32[1,5,16,1024]{3,2,1,0:T(8,128)S(1)}, f32[1,5,16,1024]{3,2,1,0:T(8,128)S(1)}, f32[1,5,16,1024]{3,2,1,0:T(8,128)S(1)}) custom-call(f32[37]{0:T(128)S(1)} %compare_select_fusion.refs_0_, f32[16,64,4096]{2,1,0:T(8,128)} %refs_1_.7), custom_call_target="tpu_custom_call" | custom-call | flops 20971520 | bytes 4194304 | tf_op jit(solution)/shard_map/moments/pallas_call | solution.py:167
  8.5 0.1 collective-permute-start.6
  8.6 3.3 %moments.7 = (f32[1,5,16,1024]{3,2,1,0:T(8,128)S(1)}, f32[1,5,16,1024]{3,2,1,0:T(8,128)S(1)}, f32[1,5,16,1024]{3,2,1,0:T(8,128)S(1)}, f32[1,5,16,1024]{3,2,1,0:T(8,128)S(1)}) custom-call(f32[37]{0:T(128)S(1)} %compare_select_fusion.refs_0_, f32[16,64,4096]{2,1,0:T(8,128)} %refs_1_.7), custom_call_target="tpu_custom_call" | custom-call | flops 20971520 | bytes 4194304 | tf_op jit(solution)/shard_map/moments/pallas_call | solution.py:167
  11.9 3.3 %moments.5 = (f32[1,5,16,1024]{3,2,1,0:T(8,128)S(1)}, f32[1,5,16,1024]{3,2,1,0:T(8,128)S(1)}, f32[1,5,16,1024]{3,2,1,0:T(8,128)S(1)}, f32[1,5,16,1024]{3,2,1,0:T(8,128)S(1)}) custom-call(f32[37]{0:T(128)S(1)} %compare_select_fusion.refs_0_, f32[16,64,4096]{2,1,0:T(8,128)} %refs_1_.7), custom_call_target="tpu_custom_call" | custom-call | flops 20971520 | bytes 4194304 | tf_op jit(solution)/shard_map/moments/pallas_call | solution.py:167
  15.3 0.0 collective-permute-done
  15.3 0.5 collective-permute-start.5
  15.8 0.0 collective-permute-done.15
  15.8 0.1 collective-permute-start.9
  15.9 0.0 collective-permute-done.12
  15.9 0.5 collective-permute-start.8
  16.4 0.0 collective-permute-done.6
  16.4 0.2 collective-permute-start.3
  16.6 0.8 %collective-permute-done.9 = f32[1,5,16,1024]{3,2,1,0:T(8,128)S(1)} collective-permute-done((f32[1,5,16,1024]{3,2,1,0:T(8,128)S(1)}, f32[1,5,16,1024]{3,2,1,0:T(8,128)S(1)}, u32[]{:S(2)}, u32[]{:S(2)}) %collective-permute-start.9) | collective-permute-done | bytes 327712 | tf_op jit(solution)/shard_map/ppermute | solution.py:273
  17.5 1.5 %collective-permute-start.7 = (f32[5,16,1024]{2,1,0:T(8,128)S(1)}, f32[5,16,1024]{2,1,0:T(8,128)S(1)}, u32[]{:S(2)}, u32[]{:S(2)}) collective-permute-start(f32[5,16,1024]{2,1,0:T(8,128)S(1)} %add_bitcast_fusion.1), channel_id=1, source_target_pairs={{0,16},{8,24},{16,0},{24,8},{1,17},{9,25},{17,1},{25,9},{2,18},{10... | collective-permute-start | bytes 983048 | tf_op jit(solution)/shard_map/ppermute | solution.py:278
  19.0 0.9 %collective-permute-start.10 = (f32[5,16,1024]{2,1,0:T(8,128)S(1)}, f32[5,16,1024]{2,1,0:T(8,128)S(1)}, u32[]{:S(2)}, u32[]{:S(2)}) collective-permute-start(f32[5,16,1024]{2,1,0:T(8,128)S(1)} %add_bitcast_fusion), channel_id=1, source_target_pairs={{0,16},{8,24},{16,0},{24,8},{1,17},{9,25},{17,1},{25,9},{2,18},{10... | collective-permute-start | bytes 983048 | tf_op jit(solution)/shard_map/ppermute | solution.py:278
  20.0 0.0 collective-permute-done.5
  20.0 0.2 collective-permute-start.2
  20.1 7.9 %collective-permute-done.7 = f32[5,16,1024]{2,1,0:T(8,128)S(1)} collective-permute-done((f32[5,16,1024]{2,1,0:T(8,128)S(1)}, f32[5,16,1024]{2,1,0:T(8,128)S(1)}, u32[]{:S(2)}, u32[]{:S(2)}) %collective-permute-start.7) | collective-permute-done | bytes 327712 | tf_op jit(solution)/shard_map/ppermute | solution.py:278
  28.1 1.5 %collective-permute-start.4 = (f32[5,16,1024]{2,1,0:T(8,128)S(1)}, f32[5,16,1024]{2,1,0:T(8,128)S(1)}, u32[]{:S(2)}, u32[]{:S(2)}) collective-permute-start(f32[5,16,1024]{2,1,0:T(8,128)S(1)} %add_bitcast_fusion.2), channel_id=1, source_target_pairs={{0,16},{8,24},{16,0},{24,8},{1,17},{9,25},{17,1},{25,9},{2,18},{10... | collective-permute-start | bytes 983048 | tf_op jit(solution)/shard_map/ppermute | solution.py:278
  29.6 0.1 bitcast_add_fusion.1.refs_3_
  29.7 0.1 collective-permute-start.14
  29.7 5.4 %collective-permute-done.10 = f32[5,16,1024]{2,1,0:T(8,128)S(1)} collective-permute-done((f32[5,16,1024]{2,1,0:T(8,128)S(1)}, f32[5,16,1024]{2,1,0:T(8,128)S(1)}, u32[]{:S(2)}, u32[]{:S(2)}) %collective-permute-start.10) | collective-permute-done | bytes 327712 | tf_op jit(solution)/shard_map/ppermute | solution.py:278
  35.1 1.5 %collective-permute-start.13 = (f32[4,16,1024]{2,1,0:T(8,128)S(1)}, f32[4,16,1024]{2,1,0:T(8,128)S(1)}, u32[]{:S(2)}, u32[]{:S(2)}) collective-permute-start(f32[4,16,1024]{2,1,0:T(8,128)S(1)} %add_bitcast_fusion.3), channel_id=1, source_target_pairs={{0,16},{8,24},{16,0},{24,8},{1,17},{9,25},{17,1},{25,9},{2,18},{10... | collective-permute-start | bytes 786440 | tf_op jit(solution)/shard_map/ppermute | solution.py:278
  36.6 0.1 bitcast_add_fusion.refs_4_
  36.7 0.0 collective-permute-done.2
  36.7 0.6 collective-permute-start.16
  37.3 4.9 %collective-permute-done.4 = f32[5,16,1024]{2,1,0:T(8,128)S(1)} collective-permute-done((f32[5,16,1024]{2,1,0:T(8,128)S(1)}, f32[5,16,1024]{2,1,0:T(8,128)S(1)}, u32[]{:S(2)}, u32[]{:S(2)}) %collective-permute-start.4) | collective-permute-done | bytes 327712 | tf_op jit(solution)/shard_map/ppermute | solution.py:278
  42.1 0.5 collective-permute-start.18
  42.6 0.1 bitcast_add_fusion.2.refs_2_
  42.7 0.0 collective-permute-done.11
  42.7 1.6 %collective-permute-start.19 = (f32[5,16,1024]{2,1,0:T(8,128)S(1)}, f32[5,16,1024]{2,1,0:T(8,128)S(1)}, u32[]{:S(2)}, u32[]{:S(2)}) collective-permute-start(f32[5,16,1024]{2,1,0:T(8,128)S(1)} %bitcast_add_fusion.refs_4_), channel_id=1, source_target_pairs={{0,1},{1,0},{2,3},{3,2},{4,5},{5,4},{6,7},{7,6},{8,9},{9,8},{10,11... | collective-permute-start | bytes 983048 | tf_op jit(solution)/shard_map/ppermute | solution.py:283
  44.3 3.5 %collective-permute-done.13 = f32[4,16,1024]{2,1,0:T(8,128)S(1)} collective-permute-done((f32[4,16,1024]{2,1,0:T(8,128)S(1)}, f32[4,16,1024]{2,1,0:T(8,128)S(1)}, u32[]{:S(2)}, u32[]{:S(2)}) %collective-permute-start.13) | collective-permute-done | bytes 262176 | tf_op jit(solution)/shard_map/ppermute | solution.py:278
  47.7 3.4 %collective-permute-start.17 = (f32[5,16,1024]{2,1,0:T(8,128)S(1)}, f32[5,16,1024]{2,1,0:T(8,128)S(1)}, u32[]{:S(2)}, u32[]{:S(2)}) collective-permute-start(f32[5,16,1024]{2,1,0:T(8,128)S(1)} %bitcast_add_fusion.2.refs_2_), channel_id=1, source_target_pairs={{1,2},{2,1},{3,4},{4,3},{5,6},{6,5},{9,10},{10,9},{11,12},{12,11},... | collective-permute-start | bytes 983048 | tf_op jit(solution)/shard_map/ppermute | solution.py:283
  51.2 0.1 bitcast_add_fusion.3.refs_5_
  51.2 1.6 %collective-permute-start.1 = (f32[8,128]{1,0:T(8,128)S(1)}, f32[8,128]{1,0:T(8,128)S(1)}, u32[]{:S(2)}, u32[]{:S(2)}) collective-permute-start(f32[8,128]{1,0:T(8,128)S(1)} %add.108), channel_id=1, source_target_pairs={{0,16},{8,24},{16,0},{24,8},{1,17},{9,25},{17,1},{25,9},{2,18},{10... | collective-permute-start | bytes 12296 | tf_op jit(solution)/shard_map/ppermute | solution.py:288
  52.8 3.3 %collective-permute-start.20 = (f32[4,16,1024]{2,1,0:T(8,128)S(1)}, f32[4,16,1024]{2,1,0:T(8,128)S(1)}, u32[]{:S(2)}, u32[]{:S(2)}) collective-permute-start(f32[4,16,1024]{2,1,0:T(8,128)S(1)} %bitcast_add_fusion.3.refs_5_), channel_id=1, source_target_pairs={{1,2},{2,1},{3,4},{4,3},{5,6},{6,5},{9,10},{10,9},{11,12},{12,11},... | collective-permute-start | bytes 786440 | tf_op jit(solution)/shard_map/ppermute | solution.py:283
  56.1 3.4 %collective-permute-start.21 = (f32[1,16,1024]{2,1,0:T(8,128)S(1)}, f32[1,16,1024]{2,1,0:T(8,128)S(1)}, u32[]{:S(2)}, u32[]{:S(2)}) collective-permute-start(f32[1,16,1024]{2,1,0:T(8,128)S(1)} %bitcast_add_fusion.4.refs_6_), channel_id=1, source_target_pairs={{1,2},{2,1},{3,4},{4,3},{5,6},{6,5},{9,10},{10,9},{11,12},{12,11},... | collective-permute-start | bytes 196616 | tf_op jit(solution)/shard_map/ppermute | solution.py:283
  59.6 7.2 %collective-permute-done.18.refs_8_ = f32[5,16,1024]{2,1,0:T(8,128)S(1)} collective-permute-done((f32[5,16,1024]{2,1,0:T(8,128)S(1)}, f32[5,16,1024]{2,1,0:T(8,128)S(1)}, u32[]{:S(2)}, u32[]{:S(2)}) %collective-permute-start.18) | collective-permute-done | bytes 327712 | tf_op jit(solution)/shard_map/ppermute | solution.py:283
  66.7 5.0 %collective-permute-done.19.refs_9_ = f32[5,16,1024]{2,1,0:T(8,128)S(1)} collective-permute-done((f32[5,16,1024]{2,1,0:T(8,128)S(1)}, f32[5,16,1024]{2,1,0:T(8,128)S(1)}, u32[]{:S(2)}, u32[]{:S(2)}) %collective-permute-start.19) | collective-permute-done | bytes 327712 | tf_op jit(solution)/shard_map/ppermute | solution.py:283
  71.7 0.0 collective-permute-done.17.refs_7_
  71.7 2.2 %inner_rows.1 = (f32[5,64,1024]{2,1,0:T(8,128)}, f32[5,16,1024]{2,1,0:T(8,128)S(1)}) custom-call(f32[37]{0:T(128)S(1)} %compare_select_fusion.refs_0_, f32[8,128]{1,0:T(8,128)S(1)} %add.109.refs_1_, f32[5,16,1024]{2,1,0:T(8,128)S(1)} %bitcast_add_fusion.2.refs_2_, f32[5,16,1024]{2,1,0:T(8,128)S(1)} %bitcast_add_fusion.1.refs_3_, ...), custom_call_target="tpu_custom_call" | custom-call | tf_op jit(solution)/shard_map/inner_rows/pallas_call | solution.py:302
  73.9 1.5 %edge_rows.1 = f32[5,64,1024]{2,1,0:T(8,128)} custom-call(f32[37]{0:T(128)S(1)} %compare_select_fusion.refs_0_, f32[8,128]{1,0:T(8,128)S(1)} %add.109.refs_1_, f32[5,16,1024]{2,1,0:T(8,128)S(1)} %get-tuple-element.49.refs_2_, f32[4,16,1024]{2,1,0:T(8,128)S(1)} %collective-permute-done.20.refs_3_, ...), custom_call_target="tpu_custom_call", output_to_operand_aliasing={{}: (5, {})} | custom-call | tf_op jit(solution)/shard_map/edge_rows/pallas_call | solution.py:312
  (15 shorter events, 0.2 us)
Async XLA Ops:
  4.1 11.7 %collective-permute-start.15 = (f32[1,1,16,1024]{3,2,1,0:T(8,128)S(1)}, f32[1,1,16,1024]{3,2,1,0:T(8,128)S(1)}, u32[]{:S(2)}, u32[]{:S(2)}) collective-permute-start(f32[1,1,16,1024]{3,2,1,0:T(8,128)S(1)} %get-tuple-element.48), channel_id=1, source_target_pairs={{0,8},{8,0},{16,24},{24,16},{1,9},{9,1},{17,25},{25,17},{2,10},{10... | collective-permute-start | bytes 196616 | tf_op jit(solution)/shard_map/ppermute | solution.py:273
  4.2 11.7 %collective-permute-start.12 = (f32[1,4,16,1024]{3,2,1,0:T(8,128)S(1)}, f32[1,4,16,1024]{3,2,1,0:T(8,128)S(1)}, u32[]{:S(2)}, u32[]{:S(2)}) collective-permute-start(f32[1,4,16,1024]{3,2,1,0:T(8,128)S(1)} %get-tuple-element.44), channel_id=1, source_target_pairs={{0,8},{8,0},{16,24},{24,16},{1,9},{9,1},{17,25},{25,17},{2,10},{10... | collective-permute-start | bytes 786440 | tf_op jit(solution)/shard_map/ppermute | solution.py:273
  4.7 10.6 %collective-permute-start = (f32[8,128]{1,0:T(8,128)S(1)}, f32[8,128]{1,0:T(8,128)S(1)}, u32[]{:S(2)}, u32[]{:S(2)}) collective-permute-start(f32[8,128]{1,0:T(8,128)S(1)} %get-tuple-element.28), channel_id=1, source_target_pairs={{0,8},{8,0},{16,24},{24,16},{1,9},{9,1},{17,25},{25,17},{2,10},{10... | collective-permute-start | bytes 12296 | tf_op jit(solution)/shard_map/ppermute | solution.py:285
  4.7 38.0 %collective-permute-start.11 = (f32[1,4,16,1024]{3,2,1,0:T(8,128)S(1)}, f32[1,4,16,1024]{3,2,1,0:T(8,128)S(1)}, u32[]{:S(2)}, u32[]{:S(2)}) collective-permute-start(f32[1,4,16,1024]{3,2,1,0:T(8,128)S(1)} %get-tuple-element.42), channel_id=1, source_target_pairs={{0,8},{8,0},{16,24},{24,16},{1,9},{9,1},{17,25},{25,17},{2,10},{10... | collective-permute-start | bytes 786440 | tf_op jit(solution)/shard_map/ppermute | solution.py:274
  8.5 7.9 %collective-permute-start.6 = (f32[1,5,16,1024]{3,2,1,0:T(8,128)S(1)}, f32[1,5,16,1024]{3,2,1,0:T(8,128)S(1)}, u32[]{:S(2)}, u32[]{:S(2)}) collective-permute-start(f32[1,5,16,1024]{3,2,1,0:T(8,128)S(1)} %get-tuple-element.36), channel_id=1, source_target_pairs={{0,8},{8,0},{16,24},{24,16},{1,9},{9,1},{17,25},{25,17},{2,10},{10... | collective-permute-start | bytes 983048 | tf_op jit(solution)/shard_map/ppermute | solution.py:273
  15.3 4.7 %collective-permute-start.5 = (f32[1,5,16,1024]{3,2,1,0:T(8,128)S(1)}, f32[1,5,16,1024]{3,2,1,0:T(8,128)S(1)}, u32[]{:S(2)}, u32[]{:S(2)}) collective-permute-start(f32[1,5,16,1024]{3,2,1,0:T(8,128)S(1)} %get-tuple-element.34), channel_id=1, source_target_pairs={{0,8},{8,0},{16,24},{24,16},{1,9},{9,1},{17,25},{25,17},{2,10},{10... | collective-permute-start | bytes 983048 | tf_op jit(solution)/shard_map/ppermute | solution.py:274
  15.8 1.7 %collective-permute-start.9 = (f32[1,5,16,1024]{3,2,1,0:T(8,128)S(1)}, f32[1,5,16,1024]{3,2,1,0:T(8,128)S(1)}, u32[]{:S(2)}, u32[]{:S(2)}) collective-permute-start(f32[1,5,16,1024]{3,2,1,0:T(8,128)S(1)} %get-tuple-element.40), channel_id=1, source_target_pairs={{0,8},{8,0},{16,24},{24,16},{1,9},{9,1},{17,25},{25,17},{2,10},{10... | collective-permute-start | bytes 983048 | tf_op jit(solution)/shard_map/ppermute | solution.py:273
  15.9 13.7 %collective-permute-start.8 = (f32[1,5,16,1024]{3,2,1,0:T(8,128)S(1)}, f32[1,5,16,1024]{3,2,1,0:T(8,128)S(1)}, u32[]{:S(2)}, u32[]{:S(2)}) collective-permute-start(f32[1,5,16,1024]{3,2,1,0:T(8,128)S(1)} %get-tuple-element.38), channel_id=1, source_target_pairs={{0,8},{8,0},{16,24},{24,16},{1,9},{9,1},{17,25},{25,17},{2,10},{10... | collective-permute-start | bytes 983048 | tf_op jit(solution)/shard_map/ppermute | solution.py:274
  16.4 2.6 %collective-permute-start.3 = (f32[1,5,16,1024]{3,2,1,0:T(8,128)S(1)}, f32[1,5,16,1024]{3,2,1,0:T(8,128)S(1)}, u32[]{:S(2)}, u32[]{:S(2)}) collective-permute-start(f32[1,5,16,1024]{3,2,1,0:T(8,128)S(1)} %get-tuple-element.32), channel_id=1, source_target_pairs={{0,8},{8,0},{16,24},{24,16},{1,9},{9,1},{17,25},{25,17},{2,10},{10... | collective-permute-start | bytes 983048 | tf_op jit(solution)/shard_map/ppermute | solution.py:273
  17.5 10.6 %collective-permute-start.7 = (f32[5,16,1024]{2,1,0:T(8,128)S(1)}, f32[5,16,1024]{2,1,0:T(8,128)S(1)}, u32[]{:S(2)}, u32[]{:S(2)}) collective-permute-start(f32[5,16,1024]{2,1,0:T(8,128)S(1)} %add_bitcast_fusion.1), channel_id=1, source_target_pairs={{0,16},{8,24},{16,0},{24,8},{1,17},{9,25},{17,1},{25,9},{2,18},{10... | collective-permute-start | bytes 983048 | tf_op jit(solution)/shard_map/ppermute | solution.py:278
  19.0 16.1 %collective-permute-start.10 = (f32[5,16,1024]{2,1,0:T(8,128)S(1)}, f32[5,16,1024]{2,1,0:T(8,128)S(1)}, u32[]{:S(2)}, u32[]{:S(2)}) collective-permute-start(f32[5,16,1024]{2,1,0:T(8,128)S(1)} %add_bitcast_fusion), channel_id=1, source_target_pairs={{0,16},{8,24},{16,0},{24,8},{1,17},{9,25},{17,1},{25,9},{2,18},{10... | collective-permute-start | bytes 983048 | tf_op jit(solution)/shard_map/ppermute | solution.py:278
  20.0 16.7 %collective-permute-start.2 = (f32[1,5,16,1024]{3,2,1,0:T(8,128)S(1)}, f32[1,5,16,1024]{3,2,1,0:T(8,128)S(1)}, u32[]{:S(2)}, u32[]{:S(2)}) collective-permute-start(f32[1,5,16,1024]{3,2,1,0:T(8,128)S(1)} %get-tuple-element.30), channel_id=1, source_target_pairs={{0,8},{8,0},{16,24},{24,16},{1,9},{9,1},{17,25},{25,17},{2,10},{10... | collective-permute-start | bytes 983048 | tf_op jit(solution)/shard_map/ppermute | solution.py:274
  28.1 14.0 %collective-permute-start.4 = (f32[5,16,1024]{2,1,0:T(8,128)S(1)}, f32[5,16,1024]{2,1,0:T(8,128)S(1)}, u32[]{:S(2)}, u32[]{:S(2)}) collective-permute-start(f32[5,16,1024]{2,1,0:T(8,128)S(1)} %add_bitcast_fusion.2), channel_id=1, source_target_pairs={{0,16},{8,24},{16,0},{24,8},{1,17},{9,25},{17,1},{25,9},{2,18},{10... | collective-permute-start | bytes 983048 | tf_op jit(solution)/shard_map/ppermute | solution.py:278
  29.7 21.6 %collective-permute-start.14 = (f32[1,1,16,1024]{3,2,1,0:T(8,128)S(1)}, f32[1,1,16,1024]{3,2,1,0:T(8,128)S(1)}, u32[]{:S(2)}, u32[]{:S(2)}) collective-permute-start(f32[1,1,16,1024]{3,2,1,0:T(8,128)S(1)} %get-tuple-element.46), channel_id=1, source_target_pairs={{0,8},{8,0},{16,24},{24,16},{1,9},{9,1},{17,25},{25,17},{2,10},{10... | collective-permute-start | bytes 196616 | tf_op jit(solution)/shard_map/ppermute | solution.py:274
  35.1 12.6 %collective-permute-start.13 = (f32[4,16,1024]{2,1,0:T(8,128)S(1)}, f32[4,16,1024]{2,1,0:T(8,128)S(1)}, u32[]{:S(2)}, u32[]{:S(2)}) collective-permute-start(f32[4,16,1024]{2,1,0:T(8,128)S(1)} %add_bitcast_fusion.3), channel_id=1, source_target_pairs={{0,16},{8,24},{16,0},{24,8},{1,17},{9,25},{17,1},{25,9},{2,18},{10... | collective-permute-start | bytes 786440 | tf_op jit(solution)/shard_map/ppermute | solution.py:278
  36.7 16.1 %collective-permute-start.16 = (f32[1,16,1024]{2,1,0:T(8,128)S(1)}, f32[1,16,1024]{2,1,0:T(8,128)S(1)}, u32[]{:S(2)}, u32[]{:S(2)}) collective-permute-start(f32[1,16,1024]{2,1,0:T(8,128)S(1)} %add_bitcast_fusion.4), channel_id=1, source_target_pairs={{0,16},{8,24},{16,0},{24,8},{1,17},{9,25},{17,1},{25,9},{2,18},{10... | collective-permute-start | bytes 196616 | tf_op jit(solution)/shard_map/ppermute | solution.py:278
  42.1 24.6 %collective-permute-start.18 = (f32[5,16,1024]{2,1,0:T(8,128)S(1)}, f32[5,16,1024]{2,1,0:T(8,128)S(1)}, u32[]{:S(2)}, u32[]{:S(2)}) collective-permute-start(f32[5,16,1024]{2,1,0:T(8,128)S(1)} %bitcast_add_fusion.1.refs_3_), channel_id=1, source_target_pairs={{0,1},{1,0},{2,3},{3,2},{4,5},{5,4},{6,7},{7,6},{8,9},{9,8},{10,11... | collective-permute-start | bytes 983048 | tf_op jit(solution)/shard_map/ppermute | solution.py:283
  42.7 29.0 %collective-permute-start.19 = (f32[5,16,1024]{2,1,0:T(8,128)S(1)}, f32[5,16,1024]{2,1,0:T(8,128)S(1)}, u32[]{:S(2)}, u32[]{:S(2)}) collective-permute-start(f32[5,16,1024]{2,1,0:T(8,128)S(1)} %bitcast_add_fusion.refs_4_), channel_id=1, source_target_pairs={{0,1},{1,0},{2,3},{3,2},{4,5},{5,4},{6,7},{7,6},{8,9},{9,8},{10,11... | collective-permute-start | bytes 983048 | tf_op jit(solution)/shard_map/ppermute | solution.py:283
  47.7 24.0 %collective-permute-start.17 = (f32[5,16,1024]{2,1,0:T(8,128)S(1)}, f32[5,16,1024]{2,1,0:T(8,128)S(1)}, u32[]{:S(2)}, u32[]{:S(2)}) collective-permute-start(f32[5,16,1024]{2,1,0:T(8,128)S(1)} %bitcast_add_fusion.2.refs_2_), channel_id=1, source_target_pairs={{1,2},{2,1},{3,4},{4,3},{5,6},{6,5},{9,10},{10,9},{11,12},{12,11},... | collective-permute-start | bytes 983048 | tf_op jit(solution)/shard_map/ppermute | solution.py:283
  51.2 4.9 %collective-permute-start.1 = (f32[8,128]{1,0:T(8,128)S(1)}, f32[8,128]{1,0:T(8,128)S(1)}, u32[]{:S(2)}, u32[]{:S(2)}) collective-permute-start(f32[8,128]{1,0:T(8,128)S(1)} %add.108), channel_id=1, source_target_pairs={{0,16},{8,24},{16,0},{24,8},{1,17},{9,25},{17,1},{25,9},{2,18},{10... | collective-permute-start | bytes 12296 | tf_op jit(solution)/shard_map/ppermute | solution.py:288
  52.8 21.1 %collective-permute-start.20 = (f32[4,16,1024]{2,1,0:T(8,128)S(1)}, f32[4,16,1024]{2,1,0:T(8,128)S(1)}, u32[]{:S(2)}, u32[]{:S(2)}) collective-permute-start(f32[4,16,1024]{2,1,0:T(8,128)S(1)} %bitcast_add_fusion.3.refs_5_), channel_id=1, source_target_pairs={{1,2},{2,1},{3,4},{4,3},{5,6},{6,5},{9,10},{10,9},{11,12},{12,11},... | collective-permute-start | bytes 786440 | tf_op jit(solution)/shard_map/ppermute | solution.py:283
  56.1 17.8 %collective-permute-start.21 = (f32[1,16,1024]{2,1,0:T(8,128)S(1)}, f32[1,16,1024]{2,1,0:T(8,128)S(1)}, u32[]{:S(2)}, u32[]{:S(2)}) collective-permute-start(f32[1,16,1024]{2,1,0:T(8,128)S(1)} %bitcast_add_fusion.4.refs_6_), channel_id=1, source_target_pairs={{1,2},{2,1},{3,4},{4,3},{5,6},{6,5},{9,10},{10,9},{11,12},{12,11},... | collective-permute-start | bytes 196616 | tf_op jit(solution)/shard_map/ppermute | solution.py:283

commit v3 on v2

--- a/solution.py
+++ b/solution.py
@@ -207,7 +207,7 @@
 
 
 def inner_kernel(values, total, *refs, chans, groups, half, bounds):
-    *pieces, out, rest = refs
+    *pieces, out, rest, marks = refs
     odd = lax.axis_index("slab") % 2
     below = odd if half == "far" else 1 - odd
     rows, late = out.shape[1], rest.shape[1]
@@ -220,23 +220,28 @@
             if low <= power < low + piece.shape[0]
         ]
         result = banded(distance, reach, jnp.concatenate(parts, axis=0))
-        out[power] = result * scale_of(total, reach)
+        scale = scale_of(total, reach)
+        marks[power : power + 1] = jnp.full((1, LANES), reach, jnp.int32).astype(jnp.float32)
+        marks[ROWS + power : ROWS + power + 1] = jnp.broadcast_to(scale, (1, LANES))
+        out[power] = result * scale
         rest[power] = jnp.where(below == 1, result[rows - late :], result[:late])
 
 
-def edge_kernel(values, total, rest, *refs, chans, groups, starts):
+def edge_kernel(rest, marks, *refs, groups, starts):
     *lasts, _, out, edge, sent = refs
     odd = lax.axis_index("slab") % 2
     slab_rows, late = out.shape[1], rest.shape[1]
     below = odd if groups[0][0] == "far" else 1 - odd
     first_row = pl.multiple_of(jnp.where(below == 1, slab_rows - late, 0), ROWS)
     distance = window((late, ROWS * len(groups)), groups, first_row, slab_rows, odd)
+    distance = distance.astype(jnp.float32)
     copies = []
     for power in range(MOMENTS):
-        reach = values[2 * chans + power].astype(jnp.int32)
+        reach = marks[power : power + 1, : distance.shape[1]]
+        scale = marks[ROWS + power : ROWS + power + 1, 0:1]
         index = max(index for index, start in enumerate(starts) if start <= power)
         last = lasts[index][power - starts[index]]
-        edge[power] = (rest[power] + banded(distance, reach, last)) * scale_of(total, reach)
+        edge[power] = (rest[power] + banded(distance, reach, last)) * scale
         copies.append(
             pltpu.make_async_copy(edge.at[power], out.at[power, pl.ds(first_row, late), :], sent.at[power])
         )
@@ -299,31 +304,35 @@
     edges = covers[-1][0]
     late = len(edges) * ROWS
     shape = jax.ShapeDtypeStruct((MOMENTS, slab_rows, span), jnp.float32)
-    result, rest = pl.pallas_call(
+    result, rest, marks = pl.pallas_call(
         lambda *refs: inner_kernel(
             *refs, chans=chans, groups=groups, half=edges[0][0], bounds=bounds
         ),
         in_specs=[smem, vmem] + [vmem] * len(pieces),
-        out_specs=(vmem, vmem),
-        out_shape=(shape, jax.ShapeDtypeStruct((MOMENTS, late, span), jnp.float32)),
+        out_specs=(vmem, vmem, vmem),
+        out_shape=(
+            shape,
+            jax.ShapeDtypeStruct((MOMENTS, late, span), jnp.float32),
+            jax.ShapeDtypeStruct((2 * ROWS, LANES), jnp.float32),
+        ),
         compiler_params=pltpu.CompilerParams(vmem_limit_bytes=16 * 2**20),
         name="inner_rows",
     )(values, total, *pieces)
     return pl.pallas_call(
         lambda *refs: edge_kernel(
-            *refs, chans=chans, groups=[(*band, False) for band in edges], starts=starts
+            *refs, groups=[(*band, False) for band in edges], starts=starts
         ),
-        in_specs=[smem, vmem, vmem] + [vmem] * last + [anywhere],
+        in_specs=[vmem, vmem] + [vmem] * last + [anywhere],
         out_specs=anywhere,
         out_shape=shape,
         scratch_shapes=[
             pltpu.VMEM((MOMENTS, late, span), jnp.float32),
             pltpu.SemaphoreType.DMA((MOMENTS,)),
         ],
-        input_output_aliases={3 + last: 0},
+        input_output_aliases={2 + last: 0},
         compiler_params=pltpu.CompilerParams(vmem_limit_bytes=16 * 2**20),
         name="edge_rows",
-    )(values, total, rest, *arrived[-last:], result)
+    )(rest, marks, *arrived[-last:], result)
 
 
 def solution(mesh):

time: 76.1 us -> 75.6 us (level)
  no operation moved by 1% of the time
where the time goes in v3:
time: 75.6 us; the launch traced here: 74.9 us
  waiting for transfers between devices  34.7 us (46%)
  starting transfers between devices  22.4 us (30%)
  Pallas kernels  16.4 us (22%)
  other arithmetic  1.2 us (2%)
    ppermute x5, waiting for transfers between devices, body(): came = lax.ppermute(sent, 'chan', hop)  21.6 us
    pallas_call x4, Pallas kernels, moments_of(): pl.pallas_call(lambda *refs: moments_kernel(*refs, bands=bands, pieces=pi...  13.2 us
    ppermute x5, starting transfers between devices, body(): arrived.append(lax.ppermute(kept, 'slab', pairs[half]))  12.2 us
    ppermute x5, waiting for transfers between devices, body(): arrived.append(lax.ppermute(kept, 'slab', pairs[half]))  12.2 us
    ppermute x5, starting transfers between devices, body(): came = lax.ppermute(sent, 'chan', hop)  5.96 us
    pallas_call x1, Pallas kernels, body(): pl.pallas_call(lambda *refs: inner_kernel(*refs, chans=chans, groups=grou...  2.2 us
    ppermute x5, starting transfers between devices, body(): got_kept = lax.ppermute(give_kept, 'chan', swap)  1.63 us
    ppermute x1, starting transfers between devices, body(): total = total + lax.ppermute(passed, 'chan', hop)  1.56 us
  transfers between devices with their start and end apart: 22, of which 7 were waited for; matrix products, arithmetic and copies ran while one was open for 1% of the time, Pallas kernels for 16%

profile of v3, /device:TPU:12, one launch (start us, length us, event | category | flops | bytes accessed | tf_op | source)
XLA Modules:
  0.0 74.9 jit_solution(12242594636435644472)
XLA Ops:
  0.0 0.8 %compare_select_fusion.refs_0_ = f32[37]{0:T(128)S(1)} fusion(s32[5]{0:T(128)} %param.7, s32[16]{0:T(128)} %param.5, f32[16]{0:T(128)} %param.6), kind=kLoop, calls=%fused_computation.10 | loop fusion | flops 444 | bytes 296 | tf_op jit(solution)/shard_map/jit(_where)/select_n | solution.py:265
  0.8 3.3 %moments.4 = (f32[1,4,16,1024]{3,2,1,0:T(8,128)S(1)}, f32[1,4,16,1024]{3,2,1,0:T(8,128)S(1)}, f32[1,4,16,1024]{3,2,1,0:T(8,128)S(1)}, f32[1,4,16,1024]{3,2,1,0:T...) custom-call(f32[37]{0:T(128)S(1)} %compare_select_fusion.refs_0_, ...), custom_call_target="tpu_custom_call" | custom-call | flops 20971520 | bytes 4194304 | tf_op jit(solution)/shard_map/moments/pallas_call | solution.py:167
  4.1 0.1 collective-permute-start.15
  4.2 0.5 collective-permute-start.12
  4.7 0.1 collective-permute-start
  4.7 0.4 collective-permute-start.11
  5.2 3.3 %moments.6 = (f32[1,5,16,1024]{3,2,1,0:T(8,128)S(1)}, f32[1,5,16,1024]{3,2,1,0:T(8,128)S(1)}, f32[1,5,16,1024]{3,2,1,0:T(8,128)S(1)}, f32[1,5,16,1024]{3,2,1,0:T(8,128)S(1)}) custom-call(f32[37]{0:T(128)S(1)} %compare_select_fusion.refs_0_, f32[16,64,4096]{2,1,0:T(8,128)} %refs_1_.7), custom_call_target="tpu_custom_call" | custom-call | flops 20971520 | bytes 4194304 | tf_op jit(solution)/shard_map/moments/pallas_call | solution.py:167
  8.5 0.1 collective-permute-start.6
  8.6 3.3 %moments.7 = (f32[1,5,16,1024]{3,2,1,0:T(8,128)S(1)}, f32[1,5,16,1024]{3,2,1,0:T(8,128)S(1)}, f32[1,5,16,1024]{3,2,1,0:T(8,128)S(1)}, f32[1,5,16,1024]{3,2,1,0:T(8,128)S(1)}) custom-call(f32[37]{0:T(128)S(1)} %compare_select_fusion.refs_0_, f32[16,64,4096]{2,1,0:T(8,128)} %refs_1_.7), custom_call_target="tpu_custom_call" | custom-call | flops 20971520 | bytes 4194304 | tf_op jit(solution)/shard_map/moments/pallas_call | solution.py:167
  11.9 3.3 %moments.5 = (f32[1,5,16,1024]{3,2,1,0:T(8,128)S(1)}, f32[1,5,16,1024]{3,2,1,0:T(8,128)S(1)}, f32[1,5,16,1024]{3,2,1,0:T(8,128)S(1)}, f32[1,5,16,1024]{3,2,1,0:T(8,128)S(1)}) custom-call(f32[37]{0:T(128)S(1)} %compare_select_fusion.refs_0_, f32[16,64,4096]{2,1,0:T(8,128)} %refs_1_.7), custom_call_target="tpu_custom_call" | custom-call | flops 20971520 | bytes 4194304 | tf_op jit(solution)/shard_map/moments/pallas_call | solution.py:167
  15.3 0.0 collective-permute-done
  15.3 0.5 collective-permute-start.5
  15.8 0.0 collective-permute-done.15
  15.8 0.1 collective-permute-start.9
  15.9 0.0 collective-permute-done.12
  15.9 0.5 collective-permute-start.8
  16.4 0.0 collective-permute-done.6
  16.4 0.2 collective-permute-start.3
  16.6 0.8 %collective-permute-done.9 = f32[1,5,16,1024]{3,2,1,0:T(8,128)S(1)} collective-permute-done((f32[1,5,16,1024]{3,2,1,0:T(8,128)S(1)}, f32[1,5,16,1024]{3,2,1,0:T(8,128)S(1)}, u32[]{:S(2)}, u32[]{:S(2)}) %collective-permute-start.9) | collective-permute-done | bytes 327712 | tf_op jit(solution)/shard_map/ppermute | solution.py:278
  17.5 1.5 %collective-permute-start.7 = (f32[5,16,1024]{2,1,0:T(8,128)S(1)}, f32[5,16,1024]{2,1,0:T(8,128)S(1)}, u32[]{:S(2)}, u32[]{:S(2)}) collective-permute-start(f32[5,16,1024]{2,1,0:T(8,128)S(1)} %add_bitcast_fusion.1), channel_id=1, source_target_pairs={{0,16},{8,24},{16,0},{24,8},{1,17},{9,25},{17,1},{25,9},{2,18},{10... | collective-permute-start | bytes 983048 | tf_op jit(solution)/shard_map/ppermute | solution.py:283
  19.0 0.9 %collective-permute-start.10 = (f32[5,16,1024]{2,1,0:T(8,128)S(1)}, f32[5,16,1024]{2,1,0:T(8,128)S(1)}, u32[]{:S(2)}, u32[]{:S(2)}) collective-permute-start(f32[5,16,1024]{2,1,0:T(8,128)S(1)} %add_bitcast_fusion), channel_id=1, source_target_pairs={{0,16},{8,24},{16,0},{24,8},{1,17},{9,25},{17,1},{25,9},{2,18},{10... | collective-permute-start | bytes 983048 | tf_op jit(solution)/shard_map/ppermute | solution.py:283
  20.0 0.0 collective-permute-done.5
  20.0 0.2 collective-permute-start.2
  20.1 7.9 %collective-permute-done.7 = f32[5,16,1024]{2,1,0:T(8,128)S(1)} collective-permute-done((f32[5,16,1024]{2,1,0:T(8,128)S(1)}, f32[5,16,1024]{2,1,0:T(8,128)S(1)}, u32[]{:S(2)}, u32[]{:S(2)}) %collective-permute-start.7) | collective-permute-done | bytes 327712 | tf_op jit(solution)/shard_map/ppermute | solution.py:283
  28.1 1.5 %collective-permute-start.4 = (f32[5,16,1024]{2,1,0:T(8,128)S(1)}, f32[5,16,1024]{2,1,0:T(8,128)S(1)}, u32[]{:S(2)}, u32[]{:S(2)}) collective-permute-start(f32[5,16,1024]{2,1,0:T(8,128)S(1)} %add_bitcast_fusion.2), channel_id=1, source_target_pairs={{0,16},{8,24},{16,0},{24,8},{1,17},{9,25},{17,1},{25,9},{2,18},{10... | collective-permute-start | bytes 983048 | tf_op jit(solution)/shard_map/ppermute | solution.py:283
  29.6 0.1 bitcast_add_fusion.1.refs_3_
  29.7 0.1 collective-permute-start.14
  29.7 5.4 %collective-permute-done.10 = f32[5,16,1024]{2,1,0:T(8,128)S(1)} collective-permute-done((f32[5,16,1024]{2,1,0:T(8,128)S(1)}, f32[5,16,1024]{2,1,0:T(8,128)S(1)}, u32[]{:S(2)}, u32[]{:S(2)}) %collective-permute-start.10) | collective-permute-done | bytes 327712 | tf_op jit(solution)/shard_map/ppermute | solution.py:283
  35.1 1.5 %collective-permute-start.13 = (f32[4,16,1024]{2,1,0:T(8,128)S(1)}, f32[4,16,1024]{2,1,0:T(8,128)S(1)}, u32[]{:S(2)}, u32[]{:S(2)}) collective-permute-start(f32[4,16,1024]{2,1,0:T(8,128)S(1)} %add_bitcast_fusion.3), channel_id=1, source_target_pairs={{0,16},{8,24},{16,0},{24,8},{1,17},{9,25},{17,1},{25,9},{2,18},{10... | collective-permute-start | bytes 786440 | tf_op jit(solution)/shard_map/ppermute | solution.py:283
  36.6 0.1 bitcast_add_fusion.refs_4_
  36.7 0.0 collective-permute-done.2
  36.7 0.6 collective-permute-start.16
  37.3 4.9 %collective-permute-done.4 = f32[5,16,1024]{2,1,0:T(8,128)S(1)} collective-permute-done((f32[5,16,1024]{2,1,0:T(8,128)S(1)}, f32[5,16,1024]{2,1,0:T(8,128)S(1)}, u32[]{:S(2)}, u32[]{:S(2)}) %collective-permute-start.4) | collective-permute-done | bytes 327712 | tf_op jit(solution)/shard_map/ppermute | solution.py:283
  42.1 0.5 collective-permute-start.18
  42.6 0.1 bitcast_add_fusion.2.refs_2_
  42.7 0.0 collective-permute-done.11
  42.7 1.6 %collective-permute-start.19 = (f32[5,16,1024]{2,1,0:T(8,128)S(1)}, f32[5,16,1024]{2,1,0:T(8,128)S(1)}, u32[]{:S(2)}, u32[]{:S(2)}) collective-permute-start(f32[5,16,1024]{2,1,0:T(8,128)S(1)} %bitcast_add_fusion.refs_4_), channel_id=1, source_target_pairs={{0,1},{1,0},{2,3},{3,2},{4,5},{5,4},{6,7},{7,6},{8,9},{9,8},{10,11... | collective-permute-start | bytes 983048 | tf_op jit(solution)/shard_map/ppermute | solution.py:288
  44.3 3.5 %collective-permute-done.13 = f32[4,16,1024]{2,1,0:T(8,128)S(1)} collective-permute-done((f32[4,16,1024]{2,1,0:T(8,128)S(1)}, f32[4,16,1024]{2,1,0:T(8,128)S(1)}, u32[]{:S(2)}, u32[]{:S(2)}) %collective-permute-start.13) | collective-permute-done | bytes 262176 | tf_op jit(solution)/shard_map/ppermute | solution.py:283
  47.7 3.4 %collective-permute-start.17 = (f32[5,16,1024]{2,1,0:T(8,128)S(1)}, f32[5,16,1024]{2,1,0:T(8,128)S(1)}, u32[]{:S(2)}, u32[]{:S(2)}) collective-permute-start(f32[5,16,1024]{2,1,0:T(8,128)S(1)} %bitcast_add_fusion.2.refs_2_), channel_id=1, source_target_pairs={{1,2},{2,1},{3,4},{4,3},{5,6},{6,5},{9,10},{10,9},{11,12},{12,11},... | collective-permute-start | bytes 983048 | tf_op jit(solution)/shard_map/ppermute | solution.py:288
  51.2 0.1 bitcast_add_fusion.3.refs_5_
  51.2 1.6 %collective-permute-start.1 = (f32[8,128]{1,0:T(8,128)S(1)}, f32[8,128]{1,0:T(8,128)S(1)}, u32[]{:S(2)}, u32[]{:S(2)}) collective-permute-start(f32[8,128]{1,0:T(8,128)S(1)} %add.108), channel_id=1, source_target_pairs={{0,16},{8,24},{16,0},{24,8},{1,17},{9,25},{17,1},{25,9},{2,18},{10... | collective-permute-start | bytes 12296 | tf_op jit(solution)/shard_map/ppermute | solution.py:293
  52.8 3.3 %collective-permute-start.20 = (f32[4,16,1024]{2,1,0:T(8,128)S(1)}, f32[4,16,1024]{2,1,0:T(8,128)S(1)}, u32[]{:S(2)}, u32[]{:S(2)}) collective-permute-start(f32[4,16,1024]{2,1,0:T(8,128)S(1)} %bitcast_add_fusion.3.refs_5_), channel_id=1, source_target_pairs={{1,2},{2,1},{3,4},{4,3},{5,6},{6,5},{9,10},{10,9},{11,12},{12,11},... | collective-permute-start | bytes 786440 | tf_op jit(solution)/shard_map/ppermute | solution.py:288
  56.1 3.4 %collective-permute-start.21 = (f32[1,16,1024]{2,1,0:T(8,128)S(1)}, f32[1,16,1024]{2,1,0:T(8,128)S(1)}, u32[]{:S(2)}, u32[]{:S(2)}) collective-permute-start(f32[1,16,1024]{2,1,0:T(8,128)S(1)} %bitcast_add_fusion.4.refs_6_), channel_id=1, source_target_pairs={{1,2},{2,1},{3,4},{4,3},{5,6},{6,5},{9,10},{10,9},{11,12},{12,11},... | collective-permute-start | bytes 196616 | tf_op jit(solution)/shard_map/ppermute | solution.py:288
  59.6 7.2 %collective-permute-done.18.refs_8_ = f32[5,16,1024]{2,1,0:T(8,128)S(1)} collective-permute-done((f32[5,16,1024]{2,1,0:T(8,128)S(1)}, f32[5,16,1024]{2,1,0:T(8,128)S(1)}, u32[]{:S(2)}, u32[]{:S(2)}) %collective-permute-start.18) | collective-permute-done | bytes 327712 | tf_op jit(solution)/shard_map/ppermute | solution.py:288
  66.7 5.0 %collective-permute-done.19.refs_9_ = f32[5,16,1024]{2,1,0:T(8,128)S(1)} collective-permute-done((f32[5,16,1024]{2,1,0:T(8,128)S(1)}, f32[5,16,1024]{2,1,0:T(8,128)S(1)}, u32[]{:S(2)}, u32[]{:S(2)}) %collective-permute-start.19) | collective-permute-done | bytes 327712 | tf_op jit(solution)/shard_map/ppermute | solution.py:288
  71.7 0.0 collective-permute-done.17.refs_7_
  71.7 2.2 %inner_rows.1 = (f32[5,64,1024]{2,1,0:T(8,128)}, f32[5,16,1024]{2,1,0:T(8,128)S(1)}, f32[16,128]{1,0:T(8,128)S(1)}) custom-call(f32[37]{0:T(128)S(1)} %compare_select_fusion.refs_0_, f32[8,128]{1,0:T(8,128)S(1)} %add.109.refs_1_, f32[5,16,1024]{2,1,0:T(8,128)S(1)} %bitcast_add_fusion.2.refs_2_, f32[5,16,1024]{2,1,0:T(8,128)S(1)} %bitcast_add_fusion.1.refs_3_, ...), custom_call_target="tpu_custom_call" | custom-call | tf_op jit(solution)/shard_map/inner_rows/pallas_call | solution.py:307
  73.9 0.9 %edge_rows.1 = f32[5,64,1024]{2,1,0:T(8,128)} custom-call(f32[5,16,1024]{2,1,0:T(8,128)S(1)} %get-tuple-element.50.refs_0_, f32[16,128]{1,0:T(8,128)S(1)} %get-tuple-element.51.refs_1_, f32[4,16,1024]{2,1,0:T(8,128)S(1)} %collective-permute-done.20.refs_2_, f32[1,16,1024]{2,1,0:T(8,128)S(1)} %collective-permute-done.21.refs_3_, ...), custom_call_target="tpu_custom_call", output_to_operand_aliasing={{}: (4, {})} | custom-call | tf_op jit(solution)/shard_map/edge_rows/pallas_call | solution.py:321
  (15 shorter events, 0.2 us)
Async XLA Ops:
  4.1 11.7 %collective-permute-start.15 = (f32[1,1,16,1024]{3,2,1,0:T(8,128)S(1)}, f32[1,1,16,1024]{3,2,1,0:T(8,128)S(1)}, u32[]{:S(2)}, u32[]{:S(2)}) collective-permute-start(f32[1,1,16,1024]{3,2,1,0:T(8,128)S(1)} %get-tuple-element.49), channel_id=1, source_target_pairs={{0,8},{8,0},{16,24},{24,16},{1,9},{9,1},{17,25},{25,17},{2,10},{10... | collective-permute-start | bytes 196616 | tf_op jit(solution)/shard_map/ppermute | solution.py:278
  4.2 11.7 %collective-permute-start.12 = (f32[1,4,16,1024]{3,2,1,0:T(8,128)S(1)}, f32[1,4,16,1024]{3,2,1,0:T(8,128)S(1)}, u32[]{:S(2)}, u32[]{:S(2)}) collective-permute-start(f32[1,4,16,1024]{3,2,1,0:T(8,128)S(1)} %get-tuple-element.45), channel_id=1, source_target_pairs={{0,8},{8,0},{16,24},{24,16},{1,9},{9,1},{17,25},{25,17},{2,10},{10... | collective-permute-start | bytes 786440 | tf_op jit(solution)/shard_map/ppermute | solution.py:278
  4.7 10.6 %collective-permute-start = (f32[8,128]{1,0:T(8,128)S(1)}, f32[8,128]{1,0:T(8,128)S(1)}, u32[]{:S(2)}, u32[]{:S(2)}) collective-permute-start(f32[8,128]{1,0:T(8,128)S(1)} %get-tuple-element.29), channel_id=1, source_target_pairs={{0,8},{8,0},{16,24},{24,16},{1,9},{9,1},{17,25},{25,17},{2,10},{10... | collective-permute-start | bytes 12296 | tf_op jit(solution)/shard_map/ppermute | solution.py:290
  4.7 38.0 %collective-permute-start.11 = (f32[1,4,16,1024]{3,2,1,0:T(8,128)S(1)}, f32[1,4,16,1024]{3,2,1,0:T(8,128)S(1)}, u32[]{:S(2)}, u32[]{:S(2)}) collective-permute-start(f32[1,4,16,1024]{3,2,1,0:T(8,128)S(1)} %get-tuple-element.43), channel_id=1, source_target_pairs={{0,8},{8,0},{16,24},{24,16},{1,9},{9,1},{17,25},{25,17},{2,10},{10... | collective-permute-start | bytes 786440 | tf_op jit(solution)/shard_map/ppermute | solution.py:279
  8.5 7.9 %collective-permute-start.6 = (f32[1,5,16,1024]{3,2,1,0:T(8,128)S(1)}, f32[1,5,16,1024]{3,2,1,0:T(8,128)S(1)}, u32[]{:S(2)}, u32[]{:S(2)}) collective-permute-start(f32[1,5,16,1024]{3,2,1,0:T(8,128)S(1)} %get-tuple-element.37), channel_id=1, source_target_pairs={{0,8},{8,0},{16,24},{24,16},{1,9},{9,1},{17,25},{25,17},{2,10},{10... | collective-permute-start | bytes 983048 | tf_op jit(solution)/shard_map/ppermute | solution.py:278
  15.3 4.7 %collective-permute-start.5 = (f32[1,5,16,1024]{3,2,1,0:T(8,128)S(1)}, f32[1,5,16,1024]{3,2,1,0:T(8,128)S(1)}, u32[]{:S(2)}, u32[]{:S(2)}) collective-permute-start(f32[1,5,16,1024]{3,2,1,0:T(8,128)S(1)} %get-tuple-element.35), channel_id=1, source_target_pairs={{0,8},{8,0},{16,24},{24,16},{1,9},{9,1},{17,25},{25,17},{2,10},{10... | collective-permute-start | bytes 983048 | tf_op jit(solution)/shard_map/ppermute | solution.py:279
  15.8 1.7 %collective-permute-start.9 = (f32[1,5,16,1024]{3,2,1,0:T(8,128)S(1)}, f32[1,5,16,1024]{3,2,1,0:T(8,128)S(1)}, u32[]{:S(2)}, u32[]{:S(2)}) collective-permute-start(f32[1,5,16,1024]{3,2,1,0:T(8,128)S(1)} %get-tuple-element.41), channel_id=1, source_target_pairs={{0,8},{8,0},{16,24},{24,16},{1,9},{9,1},{17,25},{25,17},{2,10},{10... | collective-permute-start | bytes 983048 | tf_op jit(solution)/shard_map/ppermute | solution.py:278
  15.9 13.7 %collective-permute-start.8 = (f32[1,5,16,1024]{3,2,1,0:T(8,128)S(1)}, f32[1,5,16,1024]{3,2,1,0:T(8,128)S(1)}, u32[]{:S(2)}, u32[]{:S(2)}) collective-permute-start(f32[1,5,16,1024]{3,2,1,0:T(8,128)S(1)} %get-tuple-element.39), channel_id=1, source_target_pairs={{0,8},{8,0},{16,24},{24,16},{1,9},{9,1},{17,25},{25,17},{2,10},{10... | collective-permute-start | bytes 983048 | tf_op jit(solution)/shard_map/ppermute | solution.py:279
  16.4 2.6 %collective-permute-start.3 = (f32[1,5,16,1024]{3,2,1,0:T(8,128)S(1)}, f32[1,5,16,1024]{3,2,1,0:T(8,128)S(1)}, u32[]{:S(2)}, u32[]{:S(2)}) collective-permute-start(f32[1,5,16,1024]{3,2,1,0:T(8,128)S(1)} %get-tuple-element.33), channel_id=1, source_target_pairs={{0,8},{8,0},{16,24},{24,16},{1,9},{9,1},{17,25},{25,17},{2,10},{10... | collective-permute-start | bytes 983048 | tf_op jit(solution)/shard_map/ppermute | solution.py:278
  17.5 10.6 %collective-permute-start.7 = (f32[5,16,1024]{2,1,0:T(8,128)S(1)}, f32[5,16,1024]{2,1,0:T(8,128)S(1)}, u32[]{:S(2)}, u32[]{:S(2)}) collective-permute-start(f32[5,16,1024]{2,1,0:T(8,128)S(1)} %add_bitcast_fusion.1), channel_id=1, source_target_pairs={{0,16},{8,24},{16,0},{24,8},{1,17},{9,25},{17,1},{25,9},{2,18},{10... | collective-permute-start | bytes 983048 | tf_op jit(solution)/shard_map/ppermute | solution.py:283
  19.0 16.1 %collective-permute-start.10 = (f32[5,16,1024]{2,1,0:T(8,128)S(1)}, f32[5,16,1024]{2,1,0:T(8,128)S(1)}, u32[]{:S(2)}, u32[]{:S(2)}) collective-permute-start(f32[5,16,1024]{2,1,0:T(8,128)S(1)} %add_bitcast_fusion), channel_id=1, source_target_pairs={{0,16},{8,24},{16,0},{24,8},{1,17},{9,25},{17,1},{25,9},{2,18},{10... | collective-permute-start | bytes 983048 | tf_op jit(solution)/shard_map/ppermute | solution.py:283
  20.0 16.7 %collective-permute-start.2 = (f32[1,5,16,1024]{3,2,1,0:T(8,128)S(1)}, f32[1,5,16,1024]{3,2,1,0:T(8,128)S(1)}, u32[]{:S(2)}, u32[]{:S(2)}) collective-permute-start(f32[1,5,16,1024]{3,2,1,0:T(8,128)S(1)} %get-tuple-element.31), channel_id=1, source_target_pairs={{0,8},{8,0},{16,24},{24,16},{1,9},{9,1},{17,25},{25,17},{2,10},{10... | collective-permute-start | bytes 983048 | tf_op jit(solution)/shard_map/ppermute | solution.py:279
  28.1 14.0 %collective-permute-start.4 = (f32[5,16,1024]{2,1,0:T(8,128)S(1)}, f32[5,16,1024]{2,1,0:T(8,128)S(1)}, u32[]{:S(2)}, u32[]{:S(2)}) collective-permute-start(f32[5,16,1024]{2,1,0:T(8,128)S(1)} %add_bitcast_fusion.2), channel_id=1, source_target_pairs={{0,16},{8,24},{16,0},{24,8},{1,17},{9,25},{17,1},{25,9},{2,18},{10... | collective-permute-start | bytes 983048 | tf_op jit(solution)/shard_map/ppermute | solution.py:283
  29.7 21.6 %collective-permute-start.14 = (f32[1,1,16,1024]{3,2,1,0:T(8,128)S(1)}, f32[1,1,16,1024]{3,2,1,0:T(8,128)S(1)}, u32[]{:S(2)}, u32[]{:S(2)}) collective-permute-start(f32[1,1,16,1024]{3,2,1,0:T(8,128)S(1)} %get-tuple-element.47), channel_id=1, source_target_pairs={{0,8},{8,0},{16,24},{24,16},{1,9},{9,1},{17,25},{25,17},{2,10},{10... | collective-permute-start | bytes 196616 | tf_op jit(solution)/shard_map/ppermute | solution.py:279
  35.1 12.6 %collective-permute-start.13 = (f32[4,16,1024]{2,1,0:T(8,128)S(1)}, f32[4,16,1024]{2,1,0:T(8,128)S(1)}, u32[]{:S(2)}, u32[]{:S(2)}) collective-permute-start(f32[4,16,1024]{2,1,0:T(8,128)S(1)} %add_bitcast_fusion.3), channel_id=1, source_target_pairs={{0,16},{8,24},{16,0},{24,8},{1,17},{9,25},{17,1},{25,9},{2,18},{10... | collective-permute-start | bytes 786440 | tf_op jit(solution)/shard_map/ppermute | solution.py:283
  36.7 16.1 %collective-permute-start.16 = (f32[1,16,1024]{2,1,0:T(8,128)S(1)}, f32[1,16,1024]{2,1,0:T(8,128)S(1)}, u32[]{:S(2)}, u32[]{:S(2)}) collective-permute-start(f32[1,16,1024]{2,1,0:T(8,128)S(1)} %add_bitcast_fusion.4), channel_id=1, source_target_pairs={{0,16},{8,24},{16,0},{24,8},{1,17},{9,25},{17,1},{25,9},{2,18},{10... | collective-permute-start | bytes 196616 | tf_op jit(solution)/shard_map/ppermute | solution.py:283
  42.1 24.6 %collective-permute-start.18 = (f32[5,16,1024]{2,1,0:T(8,128)S(1)}, f32[5,16,1024]{2,1,0:T(8,128)S(1)}, u32[]{:S(2)}, u32[]{:S(2)}) collective-permute-start(f32[5,16,1024]{2,1,0:T(8,128)S(1)} %bitcast_add_fusion.1.refs_3_), channel_id=1, source_target_pairs={{0,1},{1,0},{2,3},{3,2},{4,5},{5,4},{6,7},{7,6},{8,9},{9,8},{10,11... | collective-permute-start | bytes 983048 | tf_op jit(solution)/shard_map/ppermute | solution.py:288
  42.7 29.0 %collective-permute-start.19 = (f32[5,16,1024]{2,1,0:T(8,128)S(1)}, f32[5,16,1024]{2,1,0:T(8,128)S(1)}, u32[]{:S(2)}, u32[]{:S(2)}) collective-permute-start(f32[5,16,1024]{2,1,0:T(8,128)S(1)} %bitcast_add_fusion.refs_4_), channel_id=1, source_target_pairs={{0,1},{1,0},{2,3},{3,2},{4,5},{5,4},{6,7},{7,6},{8,9},{9,8},{10,11... | collective-permute-start | bytes 983048 | tf_op jit(solution)/shard_map/ppermute | solution.py:288
  47.7 24.0 %collective-permute-start.17 = (f32[5,16,1024]{2,1,0:T(8,128)S(1)}, f32[5,16,1024]{2,1,0:T(8,128)S(1)}, u32[]{:S(2)}, u32[]{:S(2)}) collective-permute-start(f32[5,16,1024]{2,1,0:T(8,128)S(1)} %bitcast_add_fusion.2.refs_2_), channel_id=1, source_target_pairs={{1,2},{2,1},{3,4},{4,3},{5,6},{6,5},{9,10},{10,9},{11,12},{12,11},... | collective-permute-start | bytes 983048 | tf_op jit(solution)/shard_map/ppermute | solution.py:288
  51.2 4.9 %collective-permute-start.1 = (f32[8,128]{1,0:T(8,128)S(1)}, f32[8,128]{1,0:T(8,128)S(1)}, u32[]{:S(2)}, u32[]{:S(2)}) collective-permute-start(f32[8,128]{1,0:T(8,128)S(1)} %add.108), channel_id=1, source_target_pairs={{0,16},{8,24},{16,0},{24,8},{1,17},{9,25},{17,1},{25,9},{2,18},{10... | collective-permute-start | bytes 12296 | tf_op jit(solution)/shard_map/ppermute | solution.py:293
  52.8 21.1 %collective-permute-start.20 = (f32[4,16,1024]{2,1,0:T(8,128)S(1)}, f32[4,16,1024]{2,1,0:T(8,128)S(1)}, u32[]{:S(2)}, u32[]{:S(2)}) collective-permute-start(f32[4,16,1024]{2,1,0:T(8,128)S(1)} %bitcast_add_fusion.3.refs_5_), channel_id=1, source_target_pairs={{1,2},{2,1},{3,4},{4,3},{5,6},{6,5},{9,10},{10,9},{11,12},{12,11},... | collective-permute-start | bytes 786440 | tf_op jit(solution)/shard_map/ppermute | solution.py:288
  56.1 17.8 %collective-permute-start.21 = (f32[1,16,1024]{2,1,0:T(8,128)S(1)}, f32[1,16,1024]{2,1,0:T(8,128)S(1)}, u32[]{:S(2)}, u32[]{:S(2)}) collective-permute-start(f32[1,16,1024]{2,1,0:T(8,128)S(1)} %bitcast_add_fusion.4.refs_6_), channel_id=1, source_target_pairs={{1,2},{2,1},{3,4},{4,3},{5,6},{6,5},{9,10},{10,9},{11,12},{12,11},... | collective-permute-start | bytes 196616 | tf_op jit(solution)/shard_map/ppermute | solution.py:288
